TPU v7x, 256 devices: a whole 4x4x8 slice. The times are simulated.
256 devices in a mesh: grp: 2 (over core), gx: 32 (over y, z), gy: 4 (over x).
Axes of the slice: x: 4, y: 4, z: 8, core: 2. Of those that a mesh axis runs over, the one named last changes fastest.
Arguments:
- coarse_ez: float32 [2048, 1024], P('gx', ('grp', 'gy')), may hold values from -6 to 6
- coarse_hx: float32 [2048, 1024], P('gx', ('grp', 'gy')), may hold values from -6 to 6
- coarse_hy: float32 [2048, 1024], P('gx', ('grp', 'gy')), may hold values from -6 to 6
- coarse_ids: int32 [2048, 1024], P('gx', ('grp', 'gy')), may hold values from 0 to 7
- mat_eps: float32 [8], replicated, may hold values from 1 to 12
- mat_sig: float32 [8], replicated, may hold values from 0 to 0.5
- fine_ez: float32 [32, 8, 32, 2304], P(None, ('grp', 'gy'), 'gx'), may hold values from -6 to 6
- fine_hx: float32 [32, 8, 32, 2304], P(None, ('grp', 'gy'), 'gx'), may hold values from -6 to 6
- fine_hy: float32 [32, 8, 32, 2304], P(None, ('grp', 'gy'), 'gx'), may hold values from -6 to 6
- fine_ids: int32 [32, 8, 32, 2304], P(None, ('grp', 'gy'), 'gx'), may hold values from 0 to 7
- boxes: int32 [32, 8, 32, 4], P('gx', ('grp', 'gy')), may hold values from 1 to 14, as said below
- src_cells: int32 [4], replicated, may hold values from 0 to 2097151
- src_wave: float32 [3, 4], replicated, may hold values from -6 to 6
- rcv_cells: int32 [128], replicated, may hold values from 0 to 2097151
Outputs:
- end_ez: float32 [2048, 1024], P('gx', ('grp', 'gy'))
- end_hx: float32 [2048, 1024], P('gx', ('grp', 'gy'))
- end_hy: float32 [2048, 1024], P('gx', ('grp', 'gy'))
- end_fine_ez: float32 [32, 8, 32, 2304], P(None, ('grp', 'gy'), 'gx')
- end_fine_hx: float32 [32, 8, 32, 2304], P(None, ('grp', 'gy'), 'gx')
- end_fine_hy: float32 [32, 8, 32, 2304], P(None, ('grp', 'gy'), 'gx')
- traces: float32 [3, 128], replicated
Inputs may be any that keep to these rules, and one draw needn't show every extreme that they name: `boxes`: each box lies one cell or more inside its tile: corner + size <= 15; sizes are 4 to 14, drawn independently for every subgrid.
All inputs are finite; a program needn't handle non-finite values.
Results may differ from a plain program's by a relative error of at most 0.00011.
Values sent between devices are 32-bit elements; how exact they have to be, the bound alone decides.
A program may use at most 64 MiB of HBM per device.

v0:
```python
import functools

import jax
import jax.numpy as jnp
from jax import lax
from jax.sharding import Mesh
from jax.sharding import PartitionSpec as P

TILE = 16
STEPS = 3
GX = ("gx_0", "gx_1")
GRP_GX_GY = ("grp", "gx_0", "gx_1", "gy")


COURANT = 0.5
HCOEF = 0.5


def with_halo(shard, sides, width):
    edges = {}
    for axis, dim in sides:
        size, length = (lax.axis_size(axis), shard.shape[dim])
        up = [(i, (i + 1) % size) for i in range(size - 1)]
        last = lax.slice_in_dim(shard, length - width, length, axis=dim)
        initial = lax.slice_in_dim(shard, 0, width, axis=dim)
        edges[dim] = (
            lax.ppermute(last, axis, up),
            lax.ppermute(initial, axis, [(b, a) for a, b in up]),
        )
    done = []
    for _, dim in sides:
        low, high = edges[dim]
        around = [(width, width) if d in done else (0, 0) for d in range(shard.ndim)]
        shard = jnp.concatenate([jnp.pad(low, around), shard, jnp.pad(high, around)], axis=dim)
        done.append(dim)
    return shard


def sent_together(arrays, axis, split_dim, concat_dim, along):
    ends, at = ([], 0)
    for a in arrays[:-1]:
        at += a.shape[along]
        ends.append(at)
    both = jnp.concatenate(arrays, axis=along)
    return tuple(
        jnp.split(
            lax.all_to_all(both, axis, split_axis=split_dim, concat_axis=concat_dim, tiled=True),
            ends,
            axis=along,
        )
    )


def by_axis(shard, axes):
    return functools.reduce(lax.psum, axes, shard)


def coefficients(ids, eps_table, sig_table, ratio):
    damp = jnp.zeros(ids.shape, jnp.float32)
    gain = jnp.zeros(ids.shape, jnp.float32)
    for material in range(eps_table.shape[0]):
        loss = sig_table[material] / (eps_table[material] * ratio)
        hit = ids == material
        damp = jnp.where(hit, (1.0 - loss) / (1.0 + loss), damp)
        gain = jnp.where(hit, COURANT / (eps_table[material] * (1.0 + loss)), gain)
    return (damp, gain)


def box_masks(boxes, cells, scale):
    coarse_of = jnp.arange(cells, dtype=jnp.int32) // scale
    low_i = boxes[..., 0:1]
    low_j = boxes[..., 1:2]
    high_i = low_i + boxes[..., 2:3]
    high_j = low_j + boxes[..., 3:4]
    rows_in = (coarse_of >= low_i) & (coarse_of < high_i)
    cols_in = (coarse_of >= low_j) & (coarse_of < high_j)
    rows_mid = (coarse_of > low_i) & (coarse_of < high_i - 1)
    cols_mid = (coarse_of > low_j) & (coarse_of < high_j - 1)
    inbox = rows_in[..., :, None] & cols_in[..., None, :]
    middle = rows_mid[..., :, None] & cols_mid[..., None, :]
    return (inbox, middle)


def flat_masks(boxes):
    width = TILE * 3
    index = jnp.arange(width * width, dtype=jnp.int32)
    coarse_i = index // width // 3
    coarse_j = index % width // 3
    low_i = boxes[:, 0:1]
    low_j = boxes[:, 1:2]
    high_i = low_i + boxes[:, 2:3]
    high_j = low_j + boxes[:, 3:4]
    inbox = (coarse_i >= low_i) & (coarse_i < high_i) & (coarse_j >= low_j) & (coarse_j < high_j)
    middle = (
        (coarse_i > low_i) & (coarse_i < high_i - 1) & (coarse_j > low_j) & (coarse_j < high_j - 1)
    )
    return (inbox, middle)


def spread_table():
    width = TILE * 3
    index = jnp.arange(width * width, dtype=jnp.int32)
    owner = index // width // 3 * TILE + index % width // 3
    return (jnp.arange(TILE * TILE, dtype=jnp.int32)[:, None] == owner[None, :]).astype(jnp.float32)


def to_flat_tiles(field):
    rows, cols = field.shape
    along_x = rows // TILE
    along_y = cols // TILE
    shaped = field.reshape(along_x, TILE, along_y, TILE).transpose(0, 2, 1, 3)
    return shaped.reshape(1, 1, along_x * along_y, TILE * TILE)


def from_tiles(tiles, block_rows, block_cols):
    along_x = block_rows // TILE
    along_y = block_cols // TILE
    shaped = tiles.reshape(along_x, along_y, TILE, TILE).transpose(0, 2, 1, 3)
    return shaped.reshape(block_rows, block_cols)


def pad_last(array, before, after):
    widths = [(0, 0)] * (array.ndim - 1) + [(before, after)]
    return jnp.pad(array, widths)


def fine_substep(fine_ez, fine_hx, fine_hy, damp, gain, inbox, middle, border, cycle_value):
    width = TILE * 3
    column = jnp.arange(width * width, dtype=jnp.int32) % width
    ez_next_col = jnp.where(column < width - 1, pad_last(fine_ez[..., 1:], 0, 1), 0.0)
    ez_next_row = pad_last(fine_ez[..., width:], 0, width)
    fine_hx = jnp.where(inbox, fine_hx - HCOEF * (ez_next_col - fine_ez), 0.0)
    fine_hy = jnp.where(inbox, fine_hy + HCOEF * (ez_next_row - fine_ez), 0.0)
    hy_prev = pad_last(fine_hy[..., :-width], width, 0)
    hx_prev = jnp.where(column > 0, pad_last(fine_hx[..., :-1], 1, 0), 0.0)
    curl = fine_hy - hy_prev - (fine_hx - hx_prev)
    inner = damp * fine_ez + gain * curl
    fine_ez = jnp.where(middle, inner, jnp.where(border, cycle_value, 0.0))
    return (fine_ez, fine_hx, fine_hy)


def fine_round(
    fine_ez, fine_hx, fine_hy, damp, gain, inbox, middle, border, old_tiles, new_tiles, spread
):
    for sub in range(1, 4):
        weight = sub / 3.0
        mixed = (1.0 - weight) * old_tiles + weight * new_tiles
        cycle_value = jnp.dot(
            mixed, spread, precision=lax.Precision.HIGHEST, preferred_element_type=jnp.float32
        )
        fine_ez, fine_hx, fine_hy = fine_substep(
            fine_ez, fine_hx, fine_hy, damp, gain, inbox, middle, border, cycle_value
        )
    return (fine_ez, fine_hx, fine_hy)


def coarse_magnetic(ez, hx, hy):
    padded = with_halo(jnp.stack([ez, hx, hy]), ((GX, 1), (("grp", "gy"), 2)), 1)
    rows, cols = ez.shape
    hx_wide = padded[1, 1:-1, :-1] - HCOEF * (padded[0, 1:-1, 1:] - padded[0, 1:-1, :-1])
    hy_wide = padded[2, :-1, 1:-1] + HCOEF * (padded[0, 1:, 1:-1] - padded[0, :-1, 1:-1])
    first_col = (jnp.arange(cols + 1) == 0)[None, :] & (lax.axis_index(("grp", "gy")) == 0)
    first_row = (jnp.arange(rows + 1) == 0)[:, None] & (lax.axis_index(GX) == 0)
    hx_wide = jnp.where(first_col, 0.0, hx_wide)
    hy_wide = jnp.where(first_row, 0.0, hy_wide)
    curl = hy_wide[1:] - hy_wide[:-1] - (hx_wide[:, 1:] - hx_wide[:, :-1])
    return (hx_wide[:, 1:], hy_wide[1:], curl)


def shards(
    coarse_ez,
    coarse_hx,
    coarse_hy,
    coarse_ids,
    mat_eps,
    mat_sig,
    fine_ez,
    fine_hx,
    fine_hy,
    fine_ids,
    boxes,
    src_cells,
    src_wave,
    rcv_cells,
):
    rows, cols = coarse_ez.shape
    fine_shape = fine_ez.shape
    flat_cells = fine_shape[-1]
    means_shape = fine_shape[:-1] + (TILE * TILE,)
    row_start = lax.axis_index(GX) * rows
    col_start = lax.axis_index(("grp", "gy")) * cols
    all_cols = cols * lax.axis_size(("grp", "gy"))
    spread = spread_table()
    damp, gain = coefficients(coarse_ids, mat_eps, mat_sig, 1.0)
    fine_damp, fine_gain = coefficients(fine_ids.reshape(-1, flat_cells), mat_eps, mat_sig, 3.0)
    owned_boxes = lax.all_to_all(boxes, GX, split_axis=2, concat_axis=0, tiled=True).reshape(-1, 4)
    inbox, middle = flat_masks(owned_boxes)
    border = inbox & jnp.logical_not(middle)
    coarse_mid = from_tiles(box_masks(boxes, TILE, 1)[1], rows, cols)
    src_rows = (
        jnp.arange(rows, dtype=jnp.int32)[None, :] == (src_cells // all_cols - row_start)[:, None]
    ).astype(jnp.float32)
    src_cols = (
        jnp.arange(cols, dtype=jnp.int32)[None, :] == (src_cells % all_cols - col_start)[:, None]
    ).astype(jnp.float32)
    rcv_rows = (
        jnp.arange(rows, dtype=jnp.int32)[None, :] == (rcv_cells // all_cols - row_start)[:, None]
    ).astype(jnp.float32)
    rcv_cols = (
        jnp.arange(cols, dtype=jnp.int32)[None, :] == (rcv_cells % all_cols - col_start)[:, None]
    ).astype(jnp.float32)
    ez, hx, hy = (coarse_ez, coarse_hx, coarse_hy)
    field_ez = fine_ez.reshape(-1, flat_cells)
    field_hx = fine_hx.reshape(-1, flat_cells)
    field_hy = fine_hy.reshape(-1, flat_cells)
    samples = []
    for step in range(STEPS):
        hx, hy, curl = coarse_magnetic(ez, hx, hy)
        weighted = src_rows * src_wave[step][:, None]
        drive = jnp.dot(
            weighted.T,
            src_cols,
            precision=lax.Precision.HIGHEST,
            preferred_element_type=jnp.float32,
        )
        new = damp * ez + gain * curl + drive
        old_tiles, new_tiles = sent_together((to_flat_tiles(ez), to_flat_tiles(new)), GX, 2, 0, 1)
        old_tiles = old_tiles.reshape(-1, TILE * TILE)
        new_tiles = new_tiles.reshape(-1, TILE * TILE)
        field_ez, field_hx, field_hy = fine_round(
            field_ez,
            field_hx,
            field_hy,
            fine_damp,
            fine_gain,
            inbox,
            middle,
            border,
            old_tiles,
            new_tiles,
            spread,
        )
        sums = lax.dot_general(
            field_ez,
            spread,
            (((1,), (1,)), ((), ())),
            precision=lax.Precision.HIGHEST,
            preferred_element_type=jnp.float32,
        )
        means = (sums / 9.0).reshape(means_shape)
        back = lax.all_to_all(means, GX, split_axis=0, concat_axis=2, tiled=True)
        ez = jnp.where(coarse_mid, from_tiles(back, rows, cols), new)
        picked = jnp.dot(
            rcv_rows, ez, precision=lax.Precision.HIGHEST, preferred_element_type=jnp.float32
        )
        samples.append(jnp.sum(picked * rcv_cols, axis=1))
    traces = by_axis(jnp.stack(samples), GRP_GX_GY)
    return (
        ez,
        hx,
        hy,
        field_ez.reshape(fine_shape),
        field_hx.reshape(fine_shape),
        field_hy.reshape(fine_shape),
        traces,
    )


def solution(mesh):
    torus = Mesh(
        mesh.devices.reshape(mesh.shape["grp"], 4, 8, mesh.shape["gy"]),
        ("grp", "gx_0", "gx_1", "gy"),
    )
    in_specs = (
        P(GX, ("grp", "gy")),
        P(GX, ("grp", "gy")),
        P(GX, ("grp", "gy")),
        P(GX, ("grp", "gy")),
        P(),
        P(),
        P(None, ("grp", "gy"), GX, None),
        P(None, ("grp", "gy"), GX, None),
        P(None, ("grp", "gy"), GX, None),
        P(None, ("grp", "gy"), GX, None),
        P(GX, ("grp", "gy"), None, None),
        P(),
        P(),
        P(),
    )
    out_specs = (
        P(GX, ("grp", "gy")),
        P(GX, ("grp", "gy")),
        P(GX, ("grp", "gy")),
        P(None, ("grp", "gy"), GX, None),
        P(None, ("grp", "gy"), GX, None),
        P(None, ("grp", "gy"), GX, None),
        P(),
    )
    return jax.shard_map(
        shards, mesh=torus, in_specs=in_specs, out_specs=out_specs, check_vma=False
    )
```

profile of v0, /device:TPU:32, one launch (start us, length us, event | category | flops | bytes accessed | tf_op | source)
XLA Modules:
  0.0 251.2 jit_solution(6563040802566183869)
XLA Ops:
  1.4 3.8 %collective-permute-start = (f32[3,1,128]{2,1,0:T(1,128)S(1)}, f32[3,1,128]{2,1,0:T(1,128)S(1)}, u32[]{:S(2)}, u32[]{:S(2)}) collective-permute-start(f32[3,1,128]{2,1,0:T(1,128)S(1)} %get-tuple-element.78), channel_id=1, source_target_pairs={{0,4},{4,8},{8,12},{12,16},{16,20},{20,24},{24,28},{28,32},{32,36}... | collective-permute-start | bytes 4616 | tf_op jit(solution)/shard_map/ppermute | solution.py:27
  8.6 12.6 %all-to-all-start = ((s32[1,1,32,4]{3,1,0,2:T(1,128)}), s32[1,1,32,4]{3,1,0,2:T(1,128)S(1)}, u32[]{:S(2)}, u32[]{:S(2)}) async-start(s32[1,1,32,4]{3,1,0,2:T(1,128)} %copy.55), calls=%async_computation | async-start | bytes 32768 | tf_op jit(solution)/shard_map/all_to_all | solution.py:196
  23.5 4.6 %collective-permute-start.2 = (f32[3,64,1]{2,1,0:T(8,128)S(1)}, f32[3,64,1]{2,1,0:T(8,128)S(1)}, u32[]{:S(2)}, u32[]{:S(2)}) collective-permute-start(f32[3,64,1]{2,1,0:T(8,128)S(1)} %get-tuple-element.77), channel_id=1, source_target_pairs={{0,1},{1,2},{2,3},{3,128},{128,129},{129,130},{130,131},{4,5},{5,6... | collective-permute-start | bytes 2312 | tf_op jit(solution)/shard_map/ppermute | solution.py:27
  68.5 9.8 %all-to-all-start.1 = ((f32[1,2,32,256]{3,1,0,2:T(2,128)}), f32[1,2,32,256]{3,1,0,2:T(2,128)S(1)}, u32[]{:S(2)}, u32[]{:S(2)}) async-start(f32[1,2,32,256]{3,1,0,2:T(2,128)} %copy.67), calls=%async_computation.1 | async-start | bytes 131072 | tf_op jit(solution)/shard_map/all_to_all | solution.py:47
  78.3 9.3 %all-to-all-done.1 = f32[1,2,32,256]{3,1,0,2:T(2,128)S(1)} async-done(((f32[1,2,32,256]{3,1,0,2:T(2,128)}), f32[1,2,32,256]{3,1,0,2:T(2,128)S(1)}, u32[]{:S(2)}, u32[]{:S(2)}) %all-to-all-start.1) | async-done | bytes 65568 | tf_op jit(solution)/shard_map/all_to_all | solution.py:47
  94.2 4.7 %all-to-all-start.2 = ((f32[32,1,1,256]{3,2,1,0:T(1,128)}), f32[32,1,1,256]{3,2,1,0:T(1,128)S(1)}, u32[]{:S(2)}, u32[]{:S(2)}) async-start(f32[32,1,1,256]{3,2,1,0:T(1,128)} %copy.68), calls=%async_computation.2 | async-start | bytes 65536 | tf_op jit(solution)/shard_map/all_to_all | solution.py:251
  99.2 8.6 %all-to-all-done.2 = f32[32,1,1,256]{3,2,1,0:T(1,128)S(1)} async-done(((f32[32,1,1,256]{3,2,1,0:T(1,128)}), f32[32,1,1,256]{3,2,1,0:T(1,128)S(1)}, u32[]{:S(2)}, u32[]{:S(2)}) %all-to-all-start.2) | async-done | bytes 32800 | tf_op jit(solution)/shard_map/all_to_all | solution.py:251
  110.8 3.3 %collective-permute-start.5 = (f32[3,1,128]{2,1,0:T(1,128)S(1)}, f32[3,1,128]{2,1,0:T(1,128)S(1)}, u32[]{:S(2)}, u32[]{:S(2)}) collective-permute-start(f32[3,1,128]{2,1,0:T(1,128)S(1)} %get-tuple-element.75), channel_id=1, source_target_pairs={{4,0},{8,4},{12,8},{16,12},{20,16},{24,20},{28,24},{32,28},{36,32}... | collective-permute-start | bytes 4616 | tf_op jit(solution)/shard_map/ppermute | solution.py:28
  115.5 4.6 %collective-permute-start.6 = (f32[3,64,1]{2,1,0:T(8,128)S(1)}, f32[3,64,1]{2,1,0:T(8,128)S(1)}, u32[]{:S(2)}, u32[]{:S(2)}) collective-permute-start(f32[3,64,1]{2,1,0:T(8,128)S(1)} %get-tuple-element.73), channel_id=1, source_target_pairs={{0,1},{1,2},{2,3},{3,128},{128,129},{129,130},{130,131},{4,5},{5,6... | collective-permute-start | bytes 2312 | tf_op jit(solution)/shard_map/ppermute | solution.py:27
  124.0 6.1 %all-to-all-start.3 = ((f32[1,2,32,256]{3,1,0,2:T(2,128)}), f32[1,2,32,256]{3,1,0,2:T(2,128)S(1)}, u32[]{:S(2)}, u32[]{:S(2)}) async-start(f32[1,2,32,256]{3,1,0,2:T(2,128)} %copy.72), calls=%async_computation.3 | async-start | bytes 131072 | tf_op jit(solution)/shard_map/all_to_all | solution.py:47
  130.1 9.1 %all-to-all-done.3 = f32[1,2,32,256]{3,1,0,2:T(2,128)S(1)} async-done(((f32[1,2,32,256]{3,1,0,2:T(2,128)}), f32[1,2,32,256]{3,1,0,2:T(2,128)S(1)}, u32[]{:S(2)}, u32[]{:S(2)}) %all-to-all-start.3) | async-done | bytes 65568 | tf_op jit(solution)/shard_map/all_to_all | solution.py:47
  145.4 4.7 %all-to-all-start.4 = ((f32[32,1,1,256]{3,2,1,0:T(1,128)}), f32[32,1,1,256]{3,2,1,0:T(1,128)S(1)}, u32[]{:S(2)}, u32[]{:S(2)}) async-start(f32[32,1,1,256]{3,2,1,0:T(1,128)} %copy.73), calls=%async_computation.4 | async-start | bytes 65536 | tf_op jit(solution)/shard_map/all_to_all | solution.py:251
  150.4 8.6 %all-to-all-done.4 = f32[32,1,1,256]{3,2,1,0:T(1,128)S(1)} async-done(((f32[32,1,1,256]{3,2,1,0:T(1,128)}), f32[32,1,1,256]{3,2,1,0:T(1,128)S(1)}, u32[]{:S(2)}, u32[]{:S(2)}) %all-to-all-start.4) | async-done | bytes 32800 | tf_op jit(solution)/shard_map/all_to_all | solution.py:251
  159.5 2.5 %collective-permute-start.8 = (f32[3,1,128]{2,1,0:T(1,128)S(1)}, f32[3,1,128]{2,1,0:T(1,128)S(1)}, u32[]{:S(2)}, u32[]{:S(2)}) collective-permute-start(f32[3,1,128]{2,1,0:T(1,128)S(1)} %get-tuple-element.70), channel_id=1, source_target_pairs={{0,4},{4,8},{8,12},{12,16},{16,20},{20,24},{24,28},{28,32},{32,36}... | collective-permute-start | bytes 4616 | tf_op jit(solution)/shard_map/ppermute | solution.py:27
  162.0 3.3 %collective-permute-start.9 = (f32[3,1,128]{2,1,0:T(1,128)S(1)}, f32[3,1,128]{2,1,0:T(1,128)S(1)}, u32[]{:S(2)}, u32[]{:S(2)}) collective-permute-start(f32[3,1,128]{2,1,0:T(1,128)S(1)} %get-tuple-element.71), channel_id=1, source_target_pairs={{4,0},{8,4},{12,8},{16,12},{20,16},{24,20},{28,24},{32,28},{36,32}... | collective-permute-start | bytes 4616 | tf_op jit(solution)/shard_map/ppermute | solution.py:28
  166.9 5.0 %collective-permute-start.10 = (f32[3,64,1]{2,1,0:T(8,128)S(1)}, f32[3,64,1]{2,1,0:T(8,128)S(1)}, u32[]{:S(2)}, u32[]{:S(2)}) collective-permute-start(f32[3,64,1]{2,1,0:T(8,128)S(1)} %get-tuple-element.69), channel_id=1, source_target_pairs={{0,1},{1,2},{2,3},{3,128},{128,129},{129,130},{130,131},{4,5},{5,6... | collective-permute-start | bytes 2312 | tf_op jit(solution)/shard_map/ppermute | solution.py:27
  175.9 6.1 %all-to-all-start.5 = ((f32[1,2,32,256]{3,1,0,2:T(2,128)}), f32[1,2,32,256]{3,1,0,2:T(2,128)S(1)}, u32[]{:S(2)}, u32[]{:S(2)}) async-start(f32[1,2,32,256]{3,1,0,2:T(2,128)} %copy.77), calls=%async_computation.5 | async-start | bytes 131072 | tf_op jit(solution)/shard_map/all_to_all | solution.py:47
  182.3 8.9 %all-to-all-done.5 = f32[1,2,32,256]{3,1,0,2:T(2,128)S(1)} async-done(((f32[1,2,32,256]{3,1,0,2:T(2,128)}), f32[1,2,32,256]{3,1,0,2:T(2,128)S(1)}, u32[]{:S(2)}, u32[]{:S(2)}) %all-to-all-start.5) | async-done | bytes 65568 | tf_op jit(solution)/shard_map/all_to_all | solution.py:47
  197.4 4.6 %all-to-all-start.6 = ((f32[32,1,1,256]{3,2,1,0:T(1,128)}), f32[32,1,1,256]{3,2,1,0:T(1,128)S(1)}, u32[]{:S(2)}, u32[]{:S(2)}) async-start(f32[32,1,1,256]{3,2,1,0:T(1,128)} %copy.78), calls=%async_computation.6 | async-start | bytes 65536 | tf_op jit(solution)/shard_map/all_to_all | solution.py:251
  205.3 5.7 %all-to-all-done.6 = f32[32,1,1,256]{3,2,1,0:T(1,128)S(1)} async-done(((f32[32,1,1,256]{3,2,1,0:T(1,128)}), f32[32,1,1,256]{3,2,1,0:T(1,128)S(1)}, u32[]{:S(2)}, u32[]{:S(2)}) %all-to-all-start.6) | async-done | bytes 32800 | tf_op jit(solution)/shard_map/all_to_all | solution.py:251
  211.8 4.2 %psum.28 = f32[3,128]{1,0:T(4,128)S(1)} all-reduce(f32[3,128]{1,0:T(4,128)S(1)} %pad_maximum_fusion.36), channel_id=1, replica_groups=mesh['grp'=2,'gx_0'=4,'gx_1'=8,'gy'=4] {'grp'}, use_global_device_ids=true, to_apply=%region_3.4 | all-reduce | flops 384 | bytes 3072 | tf_op jit(solution)/shard_map/psum | solution.py:55
  216.0 8.8 %psum.29 = f32[3,128]{1,0:T(4,128)S(1)} all-reduce(f32[3,128]{1,0:T(4,128)S(1)} %psum.28), channel_id=1, replica_groups=mesh['grp'=2,'gx_0'=4,'gx_1'=8,'gy'=4] {'gx_0'}, use_global_device_ids=true, to_apply=%region_4.5 | all-reduce | flops 384 | bytes 3072 | tf_op jit(solution)/shard_map/psum | solution.py:55
  224.8 15.4 %psum.30 = f32[3,128]{1,0:T(4,128)S(1)} all-reduce(f32[3,128]{1,0:T(4,128)S(1)} %psum.29), channel_id=1, replica_groups=mesh['grp'=2,'gx_0'=4,'gx_1'=8,'gy'=4] {'gx_1'}, use_global_device_ids=true, to_apply=%region_5.6 | all-reduce | flops 384 | bytes 3072 | tf_op jit(solution)/shard_map/psum | solution.py:55
  240.2 11.0 %psum.31 = f32[3,128]{1,0:T(4,128)} all-reduce(f32[3,128]{1,0:T(4,128)S(1)} %psum.30), channel_id=1, replica_groups=mesh['grp'=2,'gx_0'=4,'gx_1'=8,'gy'=4] {'gy'}, use_global_device_ids=true, to_apply=%region_6.7 | all-reduce | flops 384 | bytes 3072 | tf_op jit(solution)/shard_map/psum | solution.py:55
  (198 shorter events, 52.5 us)
Async XLA Ops:
  1.4 65.0 %collective-permute-start = (f32[3,1,128]{2,1,0:T(1,128)S(1)}, f32[3,1,128]{2,1,0:T(1,128)S(1)}, u32[]{:S(2)}, u32[]{:S(2)}) collective-permute-start(f32[3,1,128]{2,1,0:T(1,128)S(1)} %get-tuple-element.78), channel_id=1, source_target_pairs={{0,4},{4,8},{8,12},{12,16},{16,20},{20,24},{24,28},{28,32},{32,36}... | collective-permute-start | bytes 4616 | tf_op jit(solution)/shard_map/ppermute | solution.py:27
  5.2 61.2 %collective-permute-start.1 = (f32[3,1,128]{2,1,0:T(1,128)S(1)}, f32[3,1,128]{2,1,0:T(1,128)S(1)}, u32[]{:S(2)}, u32[]{:S(2)}) collective-permute-start(f32[3,1,128]{2,1,0:T(1,128)S(1)} %get-tuple-element.79), channel_id=1, source_target_pairs={{4,0},{8,4},{12,8},{16,12},{20,16},{24,20},{28,24},{32,28},{36,32}... | collective-permute-start | bytes 4616 | tf_op jit(solution)/shard_map/ppermute | solution.py:28
  8.6 56.6 %all-to-all-start = ((s32[1,1,32,4]{3,1,0,2:T(1,128)}), s32[1,1,32,4]{3,1,0,2:T(1,128)S(1)}, u32[]{:S(2)}, u32[]{:S(2)}) async-start(s32[1,1,32,4]{3,1,0,2:T(1,128)} %copy.55), calls=%async_computation | async-start | bytes 32768 | tf_op jit(solution)/shard_map/all_to_all | solution.py:196
  22.0 28.2 %copy-start.16 = (s32[128]{0:T(128)S(1)}, s32[128]{0:T(128)}, u32[]{:S(2)}) copy-start(s32[128]{0:T(128)} %param.27) | copy-start | bytes 1540
  22.1 28.2 %copy-start.14 = (f32[3,4]{1,0:T(4,128)S(1)}, f32[3,4]{1,0:T(4,128)}, u32[]{:S(2)}) copy-start(f32[3,4]{1,0:T(4,128)} %param.26) | copy-start | bytes 148
  22.2 39.9 %copy-start.12 = (s32[64,128]{1,0:T(8,128)S(1)}, s32[64,128]{1,0:T(8,128)}, u32[]{:S(2)}) copy-start(s32[64,128]{1,0:T(8,128)} %param.17) | copy-start | bytes 98308
  22.2 44.9 %collective-permute-start.3 = (f32[3,64,1]{2,1,0:T(8,128)S(1)}, f32[3,64,1]{2,1,0:T(8,128)S(1)}, u32[]{:S(2)}, u32[]{:S(2)}) collective-permute-start(f32[3,64,1]{2,1,0:T(8,128)S(1)} %get-tuple-element.76), channel_id=1, source_target_pairs={{1,0},{2,1},{3,2},{128,3},{129,128},{130,129},{131,130},{5,4},{6,5... | collective-permute-start | bytes 2312 | tf_op jit(solution)/shard_map/ppermute | solution.py:28
  23.5 43.5 %collective-permute-start.2 = (f32[3,64,1]{2,1,0:T(8,128)S(1)}, f32[3,64,1]{2,1,0:T(8,128)S(1)}, u32[]{:S(2)}, u32[]{:S(2)}) collective-permute-start(f32[3,64,1]{2,1,0:T(8,128)S(1)} %get-tuple-element.77), channel_id=1, source_target_pairs={{0,1},{1,2},{2,3},{3,128},{128,129},{129,130},{130,131},{4,5},{5,6... | collective-permute-start | bytes 2312 | tf_op jit(solution)/shard_map/ppermute | solution.py:27
  30.8 31.4 %copy-start.4 = (s32[32,1,1,2304]{3,2,1,0:T(1,128)S(1)}, s32[32,1,1,2304]{3,2,1,0:T(1,128)}, u32[]{:S(2)}) copy-start(s32[32,1,1,2304]{3,2,1,0:T(1,128)} %param.23) | copy-start | bytes 884740
  68.5 19.2 %all-to-all-start.1 = ((f32[1,2,32,256]{3,1,0,2:T(2,128)}), f32[1,2,32,256]{3,1,0,2:T(2,128)S(1)}, u32[]{:S(2)}, u32[]{:S(2)}) async-start(f32[1,2,32,256]{3,1,0,2:T(2,128)} %copy.67), calls=%async_computation.1 | async-start | bytes 131072 | tf_op jit(solution)/shard_map/all_to_all | solution.py:47
  94.2 13.6 %all-to-all-start.2 = ((f32[32,1,1,256]{3,2,1,0:T(1,128)}), f32[32,1,1,256]{3,2,1,0:T(1,128)S(1)}, u32[]{:S(2)}, u32[]{:S(2)}) async-start(f32[32,1,1,256]{3,2,1,0:T(1,128)} %copy.68), calls=%async_computation.2 | async-start | bytes 65536 | tf_op jit(solution)/shard_map/all_to_all | solution.py:251
  108.3 12.4 %collective-permute-start.4 = (f32[3,1,128]{2,1,0:T(1,128)S(1)}, f32[3,1,128]{2,1,0:T(1,128)S(1)}, u32[]{:S(2)}, u32[]{:S(2)}) collective-permute-start(f32[3,1,128]{2,1,0:T(1,128)S(1)} %get-tuple-element.74), channel_id=1, source_target_pairs={{0,4},{4,8},{8,12},{12,16},{16,20},{20,24},{24,28},{28,32},{32,36}... | collective-permute-start | bytes 4616 | tf_op jit(solution)/shard_map/ppermute | solution.py:27
  110.8 9.9 %collective-permute-start.5 = (f32[3,1,128]{2,1,0:T(1,128)S(1)}, f32[3,1,128]{2,1,0:T(1,128)S(1)}, u32[]{:S(2)}, u32[]{:S(2)}) collective-permute-start(f32[3,1,128]{2,1,0:T(1,128)S(1)} %get-tuple-element.75), channel_id=1, source_target_pairs={{4,0},{8,4},{12,8},{16,12},{20,16},{24,20},{28,24},{32,28},{36,32}... | collective-permute-start | bytes 4616 | tf_op jit(solution)/shard_map/ppermute | solution.py:28
  114.2 8.4 %collective-permute-start.7 = (f32[3,64,1]{2,1,0:T(8,128)S(1)}, f32[3,64,1]{2,1,0:T(8,128)S(1)}, u32[]{:S(2)}, u32[]{:S(2)}) collective-permute-start(f32[3,64,1]{2,1,0:T(8,128)S(1)} %get-tuple-element.72), channel_id=1, source_target_pairs={{1,0},{2,1},{3,2},{128,3},{129,128},{130,129},{131,130},{5,4},{6,5... | collective-permute-start | bytes 2312 | tf_op jit(solution)/shard_map/ppermute | solution.py:28
  115.5 7.0 %collective-permute-start.6 = (f32[3,64,1]{2,1,0:T(8,128)S(1)}, f32[3,64,1]{2,1,0:T(8,128)S(1)}, u32[]{:S(2)}, u32[]{:S(2)}) collective-permute-start(f32[3,64,1]{2,1,0:T(8,128)S(1)} %get-tuple-element.73), channel_id=1, source_target_pairs={{0,1},{1,2},{2,3},{3,128},{128,129},{129,130},{130,131},{4,5},{5,6... | collective-permute-start | bytes 2312 | tf_op jit(solution)/shard_map/ppermute | solution.py:27
  124.0 15.2 %all-to-all-start.3 = ((f32[1,2,32,256]{3,1,0,2:T(2,128)}), f32[1,2,32,256]{3,1,0,2:T(2,128)S(1)}, u32[]{:S(2)}, u32[]{:S(2)}) async-start(f32[1,2,32,256]{3,1,0,2:T(2,128)} %copy.72), calls=%async_computation.3 | async-start | bytes 131072 | tf_op jit(solution)/shard_map/all_to_all | solution.py:47
  145.4 13.6 %all-to-all-start.4 = ((f32[32,1,1,256]{3,2,1,0:T(1,128)}), f32[32,1,1,256]{3,2,1,0:T(1,128)S(1)}, u32[]{:S(2)}, u32[]{:S(2)}) async-start(f32[32,1,1,256]{3,2,1,0:T(1,128)} %copy.73), calls=%async_computation.4 | async-start | bytes 65536 | tf_op jit(solution)/shard_map/all_to_all | solution.py:251
  159.5 12.6 %collective-permute-start.8 = (f32[3,1,128]{2,1,0:T(1,128)S(1)}, f32[3,1,128]{2,1,0:T(1,128)S(1)}, u32[]{:S(2)}, u32[]{:S(2)}) collective-permute-start(f32[3,1,128]{2,1,0:T(1,128)S(1)} %get-tuple-element.70), channel_id=1, source_target_pairs={{0,4},{4,8},{8,12},{12,16},{16,20},{20,24},{24,28},{28,32},{32,36}... | collective-permute-start | bytes 4616 | tf_op jit(solution)/shard_map/ppermute | solution.py:27
  162.0 10.1 %collective-permute-start.9 = (f32[3,1,128]{2,1,0:T(1,128)S(1)}, f32[3,1,128]{2,1,0:T(1,128)S(1)}, u32[]{:S(2)}, u32[]{:S(2)}) collective-permute-start(f32[3,1,128]{2,1,0:T(1,128)S(1)} %get-tuple-element.71), channel_id=1, source_target_pairs={{4,0},{8,4},{12,8},{16,12},{20,16},{24,20},{28,24},{32,28},{36,32}... | collective-permute-start | bytes 4616 | tf_op jit(solution)/shard_map/ppermute | solution.py:28
  165.6 8.7 %collective-permute-start.11 = (f32[3,64,1]{2,1,0:T(8,128)S(1)}, f32[3,64,1]{2,1,0:T(8,128)S(1)}, u32[]{:S(2)}, u32[]{:S(2)}) collective-permute-start(f32[3,64,1]{2,1,0:T(8,128)S(1)} %get-tuple-element.68), channel_id=1, source_target_pairs={{1,0},{2,1},{3,2},{128,3},{129,128},{130,129},{131,130},{5,4},{6,5... | collective-permute-start | bytes 2312 | tf_op jit(solution)/shard_map/ppermute | solution.py:28
  166.9 7.2 %collective-permute-start.10 = (f32[3,64,1]{2,1,0:T(8,128)S(1)}, f32[3,64,1]{2,1,0:T(8,128)S(1)}, u32[]{:S(2)}, u32[]{:S(2)}) collective-permute-start(f32[3,64,1]{2,1,0:T(8,128)S(1)} %get-tuple-element.69), channel_id=1, source_target_pairs={{0,1},{1,2},{2,3},{3,128},{128,129},{129,130},{130,131},{4,5},{5,6... | collective-permute-start | bytes 2312 | tf_op jit(solution)/shard_map/ppermute | solution.py:27
  175.9 15.2 %all-to-all-start.5 = ((f32[1,2,32,256]{3,1,0,2:T(2,128)}), f32[1,2,32,256]{3,1,0,2:T(2,128)S(1)}, u32[]{:S(2)}, u32[]{:S(2)}) async-start(f32[1,2,32,256]{3,1,0,2:T(2,128)} %copy.77), calls=%async_computation.5 | async-start | bytes 131072 | tf_op jit(solution)/shard_map/all_to_all | solution.py:47
  197.4 13.6 %all-to-all-start.6 = ((f32[32,1,1,256]{3,2,1,0:T(1,128)}), f32[32,1,1,256]{3,2,1,0:T(1,128)S(1)}, u32[]{:S(2)}, u32[]{:S(2)}) async-start(f32[32,1,1,256]{3,2,1,0:T(1,128)} %copy.78), calls=%async_computation.6 | async-start | bytes 65536 | tf_op jit(solution)/shard_map/all_to_all | solution.py:251
  211.4 39.7 %copy-start.9 = (f32[64,128]{1,0:T(8,128)}, f32[64,128]{1,0:T(8,128)S(1)}, u32[]{:S(2)}) copy-start(f32[64,128]{1,0:T(8,128)S(1)} %select_n.656) | copy-start | bytes 98308
  (12 other events, 56.0 us)
where the time goes:
time: 253 us; the launch traced here: 251 us
  starting transfers between devices  83.9 us (33%)
  waiting for transfers between devices  53.7 us (21%)
  blocking collectives  39.4 us (16%)
  between operations  33.7 us (13%)
  local copies, waits for them, and re-layouts  18.5 us (7%)
  matrix products  14.7 us (6%)
  other arithmetic  7.36 us (3%)
    psum x4, blocking collectives, by_axis(): return functools.reduce(lax.psum, axes, shard)  39.4 us
    all_to_all x3, waiting for transfers between devices, sent_together(): lax.all_to_all(both, axis, split_axis=split_dim, concat_axis=concat_dim,...  27.3 us
    ppermute x6, starting transfers between devices, with_halo(): lax.ppermute(last, axis, up)  23 us
    all_to_all x3, waiting for transfers between devices, shards(): back = lax.all_to_all(means, GX, split_axis=0, concat_axis=2, tiled=True)  22.9 us
    all_to_all x3, starting transfers between devices, sent_together(): lax.all_to_all(both, axis, split_axis=split_dim, concat_axis=concat_dim,...  21.9 us
    all_to_all x3, starting transfers between devices, shards(): back = lax.all_to_all(means, GX, split_axis=0, concat_axis=2, tiled=True)  13.9 us
    all_to_all x1, starting transfers between devices, shards(): lax.all_to_all(boxes, GX, split_axis=2, concat_axis=0, tiled=True)  12.6 us
    ppermute x6, starting transfers between devices, with_halo(): lax.ppermute(initial, axis, [(b, a) for a, b in up])  12.5 us
  transfers between devices with their start and end apart: 19, of which 8 were waited for; matrix products, arithmetic and copies ran while one was open for 5% of the time, Pallas kernels for 0%

commit v1 on v0

v1 whole, which is shorter than its diff:
```python
import functools

import jax
import jax.numpy as jnp
from jax import lax
from jax.experimental import pallas as pl
from jax.experimental.pallas import tpu as pltpu
from jax.sharding import PartitionSpec as P

MESH = pl.DeviceIdType.MESH
NA = 32
NB = 8
STEPS = 3
f32 = jnp.float32
i32 = jnp.int32


def lanes():
    return lax.broadcasted_iota(i32, (8, 128), 1)


def sublanes():
    return lax.broadcasted_iota(i32, (8, 128), 0)


def swap_blocks(x, sub, lg):
    for k in range(3):
        bs = (sub >> k) & 1
        bl = (lg >> k) & 1
        step = 16 << k
        down = pltpu.roll(pltpu.roll(x, 1 << k, 0), 128 - step, 1)
        up = pltpu.roll(pltpu.roll(x, 8 - (1 << k), 0), step, 1)
        x = jnp.where(bs == bl, x, jnp.where(bs == 1, down, up))
    return x


def lane_gather(x, idx):
    return jnp.take_along_axis(x, idx, axis=1)


def div3(x):
    return (x * 21846) >> 16


def div48(x):
    return div3(x >> 4)


def step_tables(eps, sig, ratio):
    loss = sig / (eps * ratio)
    return (1.0 - loss) / (1.0 + loss), 0.5 / (eps * (1.0 + loss))


def kernel(
    ez_in, hx_in, hy_in, ids_in, eps_in, sig_in, fez_in, fhx_in, fhy_in, fids_in, box_in, src_in, wave_in, rcv_in,
    ez_out, hx_out, hy_out, fez_out, fhx_out, fhy_out, tr_out,
    HE, IDS, PB, PEL, PER, E2, S1, R1, S2, R2, O1, RO1, O2, RO2, TS, TB, TS2, TG,
    FE, FX, FY, FI, FD, FG, CH, U, DB, BM, IDX, TAB, NEWC, MC,
    in_sem, halo_sem, halo_send, send_sem, recv_sem, out_sem,
):
    grp = lax.axis_index("grp")
    a = lax.axis_index("gx")
    gy = lax.axis_index("gy")
    b = grp * 4 + gy

    def dev(na, nb):
        return (nb // 4, na, nb % 4)

    am, ap = lax.rem(a + NA - 1, NA), lax.rem(a + 1, NA)
    bm, bp = lax.rem(b + NB - 1, NB), lax.rem(b + 1, NB)

    barrier = pltpu.get_barrier_semaphore()

    def signal(na, nb):
        pl.semaphore_signal(barrier, inc=1, device_id=dev(na, nb), device_id_type=MESH)

    for na in (am, ap):
        for nb in (bm, bp):
            signal(na, nb)
    for d in range(1, NB):
        signal(a, lax.rem(b + d, NB))

    def signal_gx(d, carry):
        signal(lax.rem(a + d, NA), b)
        return carry

    lax.fori_loop(1, NA, signal_gx, 0)

    loads = []
    for j, (src, dst) in enumerate((
        (ez_in, HE.at[0, pl.ds(8, 64), :]),
        (hx_in, HE.at[1, pl.ds(8, 64), :]),
        (hy_in, HE.at[2, pl.ds(8, 64), :]),
        (ids_in, IDS),
        (fids_in, FI),
        (fez_in, FE),
        (fhx_in, FX),
        (fhy_in, FY),
    )):
        copy = pltpu.make_async_copy(src, dst, in_sem.at[j])
        copy.start()
        loads.append(copy)

    lane = lanes()
    sub = sublanes()
    lg = lane >> 4

    TAB[pl.ds(0, 8), :] = jnp.ones((8, 128), f32)
    TAB[pl.ds(8, 8), :] = jnp.zeros((8, 128), f32)
    TAB[pl.ds(0, 8), pl.ds(0, 8)] = jnp.broadcast_to(eps_in[...], (8, 8))
    TAB[pl.ds(8, 8), pl.ds(0, 8)] = jnp.broadcast_to(sig_in[...], (8, 8))
    eps, sig = TAB[pl.ds(0, 8), :], TAB[pl.ds(8, 8), :]
    damp1, gain1 = step_tables(eps, sig, 1.0)
    damp3, gain3 = step_tables(eps, sig, 3.0)

    for g in range(9):
        pos = lane + 128 * g
        p = div48(pos)
        q = pos - 48 * p
        IDX[pl.ds(8 * g, 8), :] = div3(p) * 16 + div3(q)

    for copy in loads[:4]:
        copy.wait()
    HE[3, pl.ds(8, 64), :] = IDS[...].astype(f32)

    def pack1(v, carry):
        ci, h = v // 2, lax.rem(v, 2)
        for k in range(4):
            x = HE[k, pl.ds(pl.multiple_of(8 + 8 * v, 8), 8), :]
            S1[pl.ds(ci * 128 + 2 * k + h, 8, stride=16), :] = swap_blocks(x, sub, lg)
        return carry

    lax.fori_loop(0, 8, pack1, 0)
    row32 = lax.broadcasted_iota(i32, (32, 32), 0)
    col32 = lax.broadcasted_iota(i32, (32, 32), 1)
    lane32 = lax.broadcasted_iota(i32, (32, 128), 1)
    box_rows = jnp.zeros((32, 128), f32)
    for k in range(4):
        one = jnp.broadcast_to(box_in[pl.ds(k, 1), :], (32, 32)).astype(f32)
        value = jnp.sum(jnp.where(row32 == col32, one, 0.0), axis=1, keepdims=True)
        box_rows = jnp.where(lane32 == k, value, box_rows)
    S1[pl.ds(8, 32, stride=16), :] = box_rows

    lane64 = lax.broadcasted_iota(i32, (64, 128), 1)
    packed = jnp.zeros((64, 128), f32)
    for k in range(4):
        near = (lane64 - 8 * k) & 127
        x = HE[k, pl.ds(8, 64), :]
        packed = jnp.where((near < 3) | (near >= 125), pltpu.roll(x, 8 * k, 1) if k else x, packed)
    PB[...] = packed

    pl.semaphore_wait(barrier, (NA - 1) + (NB - 1) + 4)

    halos = []

    def halo(j, src, dst, na, nb):
        copy = pltpu.make_async_remote_copy(
            src_ref=src, dst_ref=dst, send_sem=halo_send.at[j], recv_sem=halo_sem.at[j],
            device_id=dev(na, nb), device_id_type=MESH,
        )
        copy.start()
        halos.append(copy)

    halo(0, HE.at[:, pl.ds(64, 8), :], HE.at[:, pl.ds(0, 8), :], ap, b)
    halo(1, HE.at[:, pl.ds(8, 8), :], HE.at[:, pl.ds(72, 8), :], am, b)
    halo(2, PB, PEL.at[pl.ds(8, 64), :], a, bp)
    halo(3, PB, PER.at[pl.ds(8, 64), :], a, bm)
    halo(4, PB.at[pl.ds(56, 8), :], PEL.at[pl.ds(0, 8), :], ap, bp)
    halo(5, PB.at[pl.ds(56, 8), :], PER.at[pl.ds(0, 8), :], ap, bm)
    halo(6, PB.at[pl.ds(0, 8), :], PEL.at[pl.ds(72, 8), :], am, bp)
    halo(7, PB.at[pl.ds(0, 8), :], PER.at[pl.ds(72, 8), :], am, bm)

    def gx_copy(j, src, dst, slot, rows, n, mine):
        return pltpu.make_async_remote_copy(
            src_ref=src.at[pl.ds(pl.multiple_of(n * slot, slot), rows), :],
            dst_ref=dst.at[pl.ds(pl.multiple_of(mine * slot, slot), rows), :],
            send_sem=send_sem.at[j], recv_sem=recv_sem.at[j],
            device_id=dev(n, b), device_id_type=MESH,
        )

    def exchange(j, src, dst, slot, rows, same=False):
        def body(d, carry):
            n = lax.rem(a + d, NA)
            pltpu.make_async_remote_copy(
                src_ref=src.at[pl.ds(0 if same else pl.multiple_of(n * slot, slot), rows), :],
                dst_ref=dst.at[pl.ds(pl.multiple_of(a * slot, slot), rows), :],
                send_sem=send_sem.at[j], recv_sem=recv_sem.at[j],
                device_id=dev(n, b), device_id_type=MESH,
            ).start()
            return carry

        lax.fori_loop(1, NA, body, 0)
        own = pl.multiple_of(a * slot, slot)
        dst[pl.ds(own, rows), :] = src[pl.ds(0 if same else own, rows), :]

    def received(j, buf, rows):
        total = (NA - 1) * rows
        return pltpu.make_async_copy(buf.at[pl.ds(0, total), :], buf.at[pl.ds(0, total), :], recv_sem.at[j])

    def sent(j, buf, rows):
        total = (NA - 1) * rows
        return pltpu.make_async_copy(buf.at[pl.ds(0, total), :], buf.at[pl.ds(0, total), :], send_sem.at[j])

    exchange(0, S1, R1, 16, 9)

    loads[4].wait()

    def fine_coef(v, carry):
        rows = pl.ds(pl.multiple_of(8 * v, 8), 8)
        ids = FI[rows, :]
        FD[rows, :] = lane_gather(damp3, ids)
        FG[rows, :] = lane_gather(gain3, ids)
        return carry

    lax.fori_loop(0, 72, fine_coef, 0)

    for copy in halos:
        copy.wait()
    lane80 = lax.broadcasted_iota(i32, (80, 128), 1)
    row80 = lax.broadcasted_iota(i32, (80, 128), 0)
    row_g = row80 + (a * 64 - 8)
    col_m = lane80 + b * 128
    col_s = jnp.where(lane80 < 64, col_m + 128, col_m - 128)
    row_ok = (row_g >= 0) & (row_g < NA * 64)
    ok_m = jnp.where(row_ok, 1.0, 0.0)
    ok_s = jnp.where(row_ok & (col_s >= 0) & (col_s < NB * 128), 1.0, 0.0)

    def sides(k):
        left, right = PEL[...], PER[...]
        if k:
            left, right = pltpu.roll(left, 128 - 8 * k, 1), pltpu.roll(right, 128 - 8 * k, 1)
        return jnp.where(lane80 >= 125, left, jnp.where(lane80 < 3, right, 0.0))

    pair_ez, pair_hx, pair_hy = ((HE[k] * ok_m, sides(k) * ok_s) for k in range(3))

    def coef80(table, ids, ok):
        parts = [lane_gather(table, ids[8 * r : 8 * r + 8, :].astype(i32)) for r in range(10)]
        return jnp.concatenate(parts, axis=0) * ok

    ids_m, ids_s = HE[3], sides(3)
    pair_damp = (coef80(damp1, ids_m, ok_m), coef80(damp1, ids_s, ok_s))
    pair_gain = (coef80(gain1, ids_m, ok_m), coef80(gain1, ids_s, ok_s))

    def right_of(x):
        m, s = pltpu.roll(x[0], 127, 1), pltpu.roll(x[1], 127, 1)
        return jnp.where(lane80 < 127, m, s), jnp.where(lane80 < 127, s, m)

    def left_of(x):
        m, s = pltpu.roll(x[0], 1, 1), pltpu.roll(x[1], 1, 1)
        return jnp.where(lane80 >= 1, m, s), jnp.where(lane80 >= 1, s, m)

    def below(x):
        return pltpu.roll(x[0], 79, 0), pltpu.roll(x[1], 79, 0)

    def above(x):
        return pltpu.roll(x[0], 1, 0), pltpu.roll(x[1], 1, 0)

    def both(fn, *pairs):
        return tuple(fn(*(p[i] for p in pairs)) for i in range(2))

    src_i = [src_in[0, k] >> 10 for k in range(4)]
    src_j = [src_in[0, k] & 1023 for k in range(4)]

    def h_step(ez, hx, hy):
        hx = both(lambda h, e, r, k: (h - 0.5 * (r - e)) * k, hx, ez, right_of(ez), (ok_m, ok_s))
        hy = both(lambda h, e, r, k: (h + 0.5 * (r - e)) * k, hy, ez, below(ez), (ok_m, ok_s))
        return hx, hy

    for n in range(2):
        pair_hx, pair_hy = h_step(pair_ez, pair_hx, pair_hy)
        drive = []
        for col in (col_m, col_s):
            total = jnp.zeros((80, 128), f32)
            for k in range(4):
                total = total + jnp.where((row_g == src_i[k]) & (col == src_j[k]), wave_in[n, k], 0.0)
            drive.append(total)
        pair_ez = both(
            lambda d, e, g, hy, hu, hx, hl, s: d * e + g * ((hy - hu) - (hx - hl)) + s,
            pair_damp, pair_ez, pair_gain, pair_hy, above(pair_hy), pair_hx, left_of(pair_hx), tuple(drive),
        )
        E2[n] = pair_ez[0][8:72, :]
    pair_hx, pair_hy = h_step(pair_ez, pair_hx, pair_hy)
    E2[2] = jnp.where((row80 & 15) == 8, above(pair_hy)[0], pair_hy[0])[8:72, :]
    E2[3] = jnp.where((lane80 & 15) == 0, left_of(pair_hx)[0], pair_hx[0])[8:72, :]

    e4, t16 = (lane >> 4) & 3, lane & 15
    frame_idx = jnp.where(
        e4 == 0, t16,
        jnp.where(e4 == 1, 112 + t16, jnp.where(e4 == 2, 16 * (t16 & 7), 16 * (t16 & 7) + 15)),
    )
    from_h1 = jnp.where(e4 == 0, 0, jnp.where(e4 == 1, 1, t16 >> 3)) == 1

    def pack2(ci, carry):
        got = []
        for k in range(4):
            halves = []
            for h in range(2):
                x = E2[k, pl.ds(pl.multiple_of(16 * ci + 8 * h, 8), 8), :]
                halves.append(lane_gather(swap_blocks(x, sub, lg), frame_idx))
            got.append(jnp.where(from_h1, halves[1], halves[0]))
        S2[pl.ds(ci * 64, 8, stride=8), :] = jnp.where(lane < 64, got[0], got[1])
        S2[pl.ds(ci * 64 + 1, 8, stride=8), :] = jnp.where((lane & 63) < 32, got[2], got[3])
        return carry

    lax.fori_loop(0, 4, pack2, 0)
    exchange(1, S2, R2, 8, 2)

    received(0, R1, 9).wait()
    for copy in loads[5:]:
        copy.wait()

    def from1(k):
        return tuple(R1[pl.ds(2 * k + h, 32, stride=16), :] for h in range(2))

    ez, hx, hy, ids_c = (from1(k) for k in range(4))

    def coef32(table, ids):
        parts = [lane_gather(table, ids[8 * r : 8 * r + 8, :].astype(i32)) for r in range(4)]
        return jnp.concatenate(parts, axis=0)

    damp = tuple(coef32(damp1, x) for x in ids_c)
    gain = tuple(coef32(gain1, x) for x in ids_c)
    NEWC[pl.ds(0, 32), :], NEWC[pl.ds(32, 32), :] = ez

    def prepare(tg, carry):
        base = tg * 144
        box = R1[pl.ds(tg * 128 + 8, 8, stride=16), :]
        lo_i, lo_j, n_i, n_j = (jnp.broadcast_to(box[:, k : k + 1], (8, 128)).astype(i32) for k in range(4))
        hi_i, hi_j = lo_i + n_i, lo_j + n_j
        old = [NEWC[pl.ds(pl.multiple_of(32 * h + 8 * tg, 8), 8), :] for h in range(2)]
        for g in range(18):
            rows = pl.ds(base + g, 8, stride=18)
            idx = IDX[pl.ds(8 * (g % 9), 8), :]
            ci = (idx >> 4) + (8 if g >= 9 else 0)
            cj = idx & 15
            inbox = (ci >= lo_i) & (ci < hi_i) & (cj >= lo_j) & (cj < hi_j)
            middle = (ci > lo_i) & (ci < hi_i - 1) & (cj > lo_j) & (cj < hi_j - 1)
            fin = jnp.where(inbox, 1.0, 0.0)
            fmid = jnp.where(middle, 1.0, 0.0)
            fbor = fin - fmid
            FX[rows, :] = FX[rows, :] * fin
            FY[rows, :] = FY[rows, :] * fin
            CH[rows, :] = 0.5 * fin
            FD[rows, :] = FD[rows, :] * fmid
            FG[rows, :] = FG[rows, :] * fmid
            BM[rows, :] = fbor
            U[rows, :] = fbor * lane_gather(old[g // 9], idx)
        return carry

    lax.fori_loop(0, 4, prepare, 0)

    mean_pos = 144 * (lane >> 4) + 3 * (lane & 15)
    mean_idx = mean_pos & 127
    mean_group = mean_pos >> 7

    def fine_round(tg, carry):
        base = tg * 144

        def at(g):
            return pl.ds(base + g, 8, stride=18)

        new = [NEWC[pl.ds(pl.multiple_of(32 * h + 8 * tg, 8), 8), :] for h in range(2)]
        for g in range(18):
            value = BM[at(g), :] * lane_gather(new[g // 9], IDX[pl.ds(8 * (g % 9), 8), :])
            DB[at(g), :] = value - U[at(g), :]
            U[at(g), :] = value

        def substep(m, carry):
            behind = (2 - m).astype(f32) * (1.0 / 3.0)
            e = FE[at(0), :]
            e1, e48 = pltpu.roll(e, 127, 1), pltpu.roll(e, 80, 1)
            x1 = y48 = None
            for g in range(18):
                if g < 17:
                    e_next = FE[at(g + 1), :]
                    n1, n48 = pltpu.roll(e_next, 127, 1), pltpu.roll(e_next, 80, 1)
                c = CH[at(g), :]
                hx_g = FX[at(g), :] - c * (jnp.where(lane < 127, e1, n1) - e)
                hy_g = FY[at(g), :] + c * (jnp.where(lane < 80, e48, n48) - e)
                FX[at(g), :] = hx_g
                FY[at(g), :] = hy_g
                rx, ry = pltpu.roll(hx_g, 1, 1), pltpu.roll(hy_g, 48, 1)
                if g == 0:
                    x1, y48 = rx, ry
                curl = (hy_g - jnp.where(lane >= 48, ry, y48)) - (hx_g - jnp.where(lane >= 1, rx, x1))
                FE[at(g), :] = FD[at(g), :] * e + FG[at(g), :] * curl + (U[at(g), :] - behind * DB[at(g), :])
                x1, y48 = rx, ry
                e, e1, e48 = e_next, n1, n48
            return carry

        lax.fori_loop(0, 3, substep, 0)

        def sums(g):
            x = FE[at(g), :]
            return x, pltpu.roll(x, 127, 1), pltpu.roll(x, 126, 1)

        for h in range(2):
            groups = [sums(9 * h + g) for g in range(9)]
            groups.append(sums(9) if h == 0 else groups[8])
            rowsum = [
                groups[g][0]
                + jnp.where(lane < 127, groups[g][1], groups[min(g + 1, 9)][1])
                + jnp.where(lane < 126, groups[g][2], groups[min(g + 1, 9)][2])
                for g in range(10)
            ]
            r48 = [pltpu.roll(x, 80, 1) for x in rowsum]
            r96 = [pltpu.roll(x, 32, 1) for x in rowsum]
            total = jnp.zeros((8, 128), f32)
            for g in range(9):
                s = rowsum[g] + jnp.where(lane < 80, r48[g], r48[g + 1]) + jnp.where(lane < 32, r96[g], r96[g + 1])
                total = jnp.where(mean_group == g, lane_gather(s, mean_idx), total)
            MC[pl.ds(pl.multiple_of(32 * h + 8 * tg, 8), 8), :] = total * (1.0 / 9.0)
        return carry

    row_in = lane32 >> 4
    col_in = lane32 & 15
    boxes = R1[pl.ds(8, 32, stride=16), :]
    lo_i, lo_j, n_i, n_j = (jnp.broadcast_to(boxes[:, k : k + 1], (32, 128)).astype(i32) for k in range(4))
    mid = tuple(
        (row_in + 8 * h > lo_i) & (row_in + 8 * h < lo_i + n_i - 1) & (col_in > lo_j) & (col_in < lo_j + n_j - 1)
        for h in range(2)
    )
    edge_col = (col_in == 0) | (col_in == 15)
    frame = (edge_col | (row_in == 0), edge_col | (row_in == 7))
    tile32 = lax.broadcasted_iota(i32, (32, 128), 0)
    my_ci, my_cj = a // 8, lax.rem(a, 8)
    src_tile, src_cell = [], []
    for k in range(4):
        i, j = src_i[k], src_j[k]
        here = ((i & 63) >> 4 == my_ci) & ((j & 127) >> 4 == my_cj) & (j >> 7 == b)
        src_tile.append(jnp.where(here, i >> 6, -1))
        src_cell.append((i & 15) * 16 + (j & 15))
    rcv = jnp.broadcast_to(rcv_in[...], (8, 128))
    ri, rj = rcv >> 10, rcv & 1023
    r_here = (((ri & 63) >> 4) == my_ci) & (((rj & 127) >> 4) == my_cj) & ((rj >> 7) == b)
    r_tile = jnp.where(r_here, ri >> 6, -1)
    r_cell = (ri & 15) * 16 + (rj & 15)
    r_idx, r_half = r_cell & 127, r_cell >> 7

    def c_right(x):
        return tuple(pltpu.roll(v, 127, 1) for v in x)

    def c_left(x):
        return tuple(pltpu.roll(v, 1, 1) for v in x)

    def c_below(x):
        y = tuple(pltpu.roll(v, 112, 1) for v in x)
        return jnp.where(lane32 < 112, y[0], y[1]), y[1]

    def c_above(x):
        y = tuple(pltpu.roll(v, 16, 1) for v in x)
        return y[0], jnp.where(lane32 >= 16, y[1], y[0])

    framed = None
    for n in range(STEPS):
        hx = both(lambda h, e, r: h - 0.5 * (r - e), hx, ez, c_right(ez))
        hy = both(lambda h, e, r: h + 0.5 * (r - e), hy, ez, c_below(ez))
        hx_left, hy_up = c_left(hx), c_above(hy)
        if n == 2:
            edge = R2[pl.ds(1, 32, stride=8), :]

            def spread(idx):
                parts = [lane_gather(edge[8 * r : 8 * r + 8, :], idx) for r in range(4)]
                return jnp.concatenate(parts, axis=0)

            w1 = tuple(spread(t16 + 16 * h) for h in range(2))
            w2 = tuple(spread(jnp.where(t16 == 15, 48, 32) + (lane >> 4) + 8 * h) for h in range(2))
            hy = (hy[0], jnp.where(row_in == 7, w1[1], hy[1]))
            hx = tuple(jnp.where(col_in == 15, w2[h], hx[h]) for h in range(2))
            hy_up = (jnp.where(row_in == 0, w1[0], hy_up[0]), hy_up[1])
            hx_left = tuple(jnp.where(col_in == 0, w2[h], hx_left[h]) for h in range(2))
            for h in range(2):
                O1[pl.ds(h, 32, stride=8), :] = hx[h]
                O1[pl.ds(2 + h, 32, stride=8), :] = hy[h]
            exchange(2, O1, RO1, 8, 4)
        drive = []
        for h in range(2):
            total = jnp.zeros((32, 128), f32)
            for k in range(4):
                total = total + jnp.where(
                    (tile32 == src_tile[k]) & (lane32 + 128 * h == src_cell[k]), wave_in[n, k], 0.0
                )
            drive.append(total)
        new = both(
            lambda d, e, g, y, yu, x, xl, s: d * e + g * ((y - yu) - (x - xl)) + s,
            damp, ez, gain, hy, hy_up, hx, hx_left, tuple(drive),
        )
        NEWC[pl.ds(0, 32), :], NEWC[pl.ds(32, 32), :] = new
        lax.fori_loop(0, 4, fine_round, 0)
        if n == 0:
            received(1, R2, 2).wait()
        if n < 2:
            rim = R2[pl.ds(0, 32, stride=8), :]
            out = []
            for h in range(2):
                r = (lane >> 4) + 8 * h
                slot = jnp.where(
                    r == 0, t16, jnp.where(r == 15, 16 + t16, jnp.where(t16 == 0, 32 + r, 48 + r))
                )
                slot = (slot & 63) + 64 * n
                parts = [lane_gather(rim[8 * q : 8 * q + 8, :], slot) for q in range(4)]
                out.append(jnp.where(frame[h], jnp.concatenate(parts, axis=0), new[h]))
            new = tuple(out)
        ez = both(lambda m, x, y: jnp.where(m, x, y), mid, (MC[pl.ds(0, 32), :], MC[pl.ds(32, 32), :]), new)
        if n == 2:
            for h in range(2):
                O2[pl.ds(h, 32, stride=8), :] = ez[h]
            exchange(3, O2, RO2, 8, 2)
        picked = jnp.zeros((8, 128), f32)
        for h in range(2):
            for q in range(4):
                got = lane_gather(ez[h][8 * q : 8 * q + 8, :], r_idx)
                picked = picked + jnp.where((r_tile == sub + 8 * q) & (r_half == h), got, 0.0)
        TS[pl.ds(n, 1), :] = jnp.sum(picked, axis=0, keepdims=True)

    for d in range(1, NB):
        n = lax.rem(b + d, NB)
        pltpu.make_async_remote_copy(
            src_ref=TS.at[pl.ds(0, 3), :],
            dst_ref=TB.at[pl.ds(pl.multiple_of(8 * b, 8), 3), :],
            send_sem=send_sem.at[4], recv_sem=recv_sem.at[4],
            device_id=dev(a, n), device_id_type=MESH,
        ).start()
    TB[pl.ds(pl.multiple_of(8 * b, 8), 3), :] = TS[pl.ds(0, 3), :]

    stores = []
    for j, (src, dst) in enumerate(((FE, fez_out), (FX, fhx_out), (FY, fhy_out))):
        copy = pltpu.make_async_copy(src, dst, out_sem.at[j])
        copy.start()
        stores.append(copy)

    seven = (NB - 1) * 3
    pltpu.make_async_copy(TB.at[pl.ds(0, seven), :], TB.at[pl.ds(0, seven), :], recv_sem.at[4]).wait()
    for n in range(STEPS):
        TS2[pl.ds(n, 1), :] = jnp.sum(TB[pl.ds(n, 8, stride=8), :], axis=0, keepdims=True)
    exchange(5, TS2, TG, 8, 3, same=True)

    received(2, RO1, 4).wait()

    def unpack(src, first, dst):
        def body(ci, carry):
            for h in range(2):
                x = src[pl.ds(ci * 64 + first + h, 8, stride=8), :]
                dst[pl.ds(pl.multiple_of(16 * ci + 8 * h, 8), 8), :] = swap_blocks(x, sub, lg)
            return carry

        lax.fori_loop(0, 4, body, 0)

    unpack(RO1, 0, hx_out)
    unpack(RO1, 2, hy_out)
    received(3, RO2, 2).wait()
    unpack(RO2, 0, ez_out)
    received(5, TG, 3).wait()
    for n in range(STEPS):
        tr_out[pl.ds(n, 1), :] = jnp.sum(TG[pl.ds(n, 32, stride=8), :], axis=0, keepdims=True)

    for copy in stores:
        copy.wait()
    for j, buf, rows in ((0, S1, 9), (1, S2, 2), (2, O1, 4), (3, O2, 2), (5, TG, 3)):
        sent(j, buf, rows).wait()
    pltpu.make_async_copy(TB.at[pl.ds(0, seven), :], TB.at[pl.ds(0, seven), :], send_sem.at[4]).wait()


def shards(
    coarse_ez, coarse_hx, coarse_hy, coarse_ids, mat_eps, mat_sig,
    fine_ez, fine_hx, fine_hy, fine_ids, boxes, src_cells, src_wave, rcv_cells,
):
    fine_shape = fine_ez.shape
    flat = (576, 128)
    anywhere = pl.BlockSpec(memory_space=pl.ANY)
    vmem = pl.BlockSpec(memory_space=pltpu.VMEM)
    smem = pl.BlockSpec(memory_space=pltpu.SMEM)
    block = jax.ShapeDtypeStruct((64, 128), f32)
    fine = jax.ShapeDtypeStruct(flat, f32)

    def v(*shape, dtype=f32):
        return pltpu.VMEM(shape, dtype)

    outs = pl.pallas_call(
        kernel,
        name="nested",
        out_shape=(block, block, block, fine, fine, fine, jax.ShapeDtypeStruct((3, 128), f32)),
        in_specs=[anywhere] * 4 + [vmem] * 2 + [anywhere] * 4 + [vmem, smem, smem, vmem],
        out_specs=(vmem, vmem, vmem, anywhere, anywhere, anywhere, vmem),
        scratch_shapes=[
            v(4, 80, 128), v(64, 128, dtype=i32), v(64, 128), v(80, 128), v(80, 128), v(4, 64, 128),
            v(512, 128), v(512, 128), v(256, 128), v(256, 128),
            v(256, 128), v(256, 128), v(256, 128), v(256, 128),
            v(8, 128), v(64, 128), v(8, 128), v(256, 128),
            v(576, 128), v(576, 128), v(576, 128), v(576, 128, dtype=i32),
            v(576, 128), v(576, 128), v(576, 128), v(576, 128), v(576, 128), v(576, 128),
            v(72, 128, dtype=i32), v(16, 128), v(64, 128), v(64, 128),
            pltpu.SemaphoreType.DMA((8,)), pltpu.SemaphoreType.DMA((8,)), pltpu.SemaphoreType.DMA((8,)),
            pltpu.SemaphoreType.DMA((6,)), pltpu.SemaphoreType.DMA((6,)), pltpu.SemaphoreType.DMA((3,)),
        ],
        compiler_params=pltpu.CompilerParams(collective_id=0, has_side_effects=True),
    )(
        coarse_ez, coarse_hx, coarse_hy, coarse_ids,
        mat_eps.reshape(1, 8), mat_sig.reshape(1, 8),
        fine_ez.reshape(flat), fine_hx.reshape(flat), fine_hy.reshape(flat), fine_ids.reshape(flat),
        boxes.reshape(32, 4).T, src_cells.reshape(1, 4), src_wave, rcv_cells.reshape(1, 128),
    )
    return outs[:3] + tuple(x.reshape(fine_shape) for x in outs[3:6]) + (outs[6],)


def solution(mesh):
    coarse = P("gx", ("grp", "gy"))
    tiles = P(None, ("grp", "gy"), "gx", None)
    in_specs = (
        coarse, coarse, coarse, coarse, P(), P(), tiles, tiles, tiles, tiles,
        P("gx", ("grp", "gy"), None, None), P(), P(), P(),
    )
    out_specs = (coarse, coarse, coarse, tiles, tiles, tiles, P())
    return jax.shard_map(shards, mesh=mesh, in_specs=in_specs, out_specs=out_specs, check_vma=False)
```

time: 253 us -> 53 us (0.21)
  the two profiles are of different devices: /device:TPU:32 before, /device:TPU:1 now
where the time goes in v1:
time: 53 us; the launch traced here: 52.7 us
  Pallas kernels  45.1 us (85%)
  local copies, waits for them, and re-layouts  6.88 us (13%)
  between operations  0.66 us (1%)
    pallas_call x1, Pallas kernels, shards(): pl.pallas_call(kernel, name='nested', out_shape=(block, block, block, fin...  45.1 us
    unnamed x17, local copies, waits for them, and re-layouts  6.88 us

profile of v1, /device:TPU:1, one launch (start us, length us, event | category | flops | bytes accessed | tf_op | source)
XLA Modules:
  0.0 52.7 jit_solution(4793858244420480829)
XLA Ops:
  0.6 45.1 %nested.1 = (f32[64,128]{1,0:T(8,128)}, f32[64,128]{1,0:T(8,128)}, f32[64,128]{1,0:T(8,128)}, f32[576,128]{1,0:T(8,128)}, f32[576,128]{1,0:T(8,128)}, /*index=5*/f32[576,128]{1,0:T(8,128)}, f32[3,128]{1,0:T(4,128)}) custom-call(f32[64,128]{1,0:T(8,128)} %ez_in.1, f32[64,128]{1,0:T(8,128)} %hx_in.1, f32[64,128]{1,0:T(8,128)} %hy_in.1, s32[64,128]{1,0:T(8,128)} %ids_in.1, ...), custom_call_target="tpu_custom_call" | custom-call | tf_op jit(solution)/shard_map/nested/pallas_call | solution.py:579
  45.8 0.0 copy-start.3
  45.8 1.4 %copy.31 = f32[64,128]{1,0:T(8,128)} copy(f32[64,128]{1,0:T(8,128)} %get-tuple-element.35) | data formatting | bytes 65536
  47.2 0.0 copy-done.3
  47.2 0.0 copy-start.2
  47.2 0.6 %copy.32 = f32[64,128]{1,0:T(8,128)} copy(f32[64,128]{1,0:T(8,128)S(1)} %copy-done.3) | data formatting | bytes 65536
  47.8 0.2 copy-done.2
  48.0 0.6 %copy.33 = f32[64,128]{1,0:T(8,128)} copy(f32[64,128]{1,0:T(8,128)S(1)} %copy-done.2) | data formatting | bytes 65536
  48.6 0.0 copy-start.1
  48.6 1.7 %copy.34 = f32[32,1,1,2304]{3,2,1,0:T(1,128)} copy(f32[32,1,1,2304]{3,2,1,0:T(1,128)} %bitcast.20) | data formatting | bytes 589824
  50.3 0.0 copy-done.1
  50.3 0.0 copy-start
  50.3 0.7 %copy.35 = f32[32,1,1,2304]{3,2,1,0:T(1,128)} copy(f32[32,1,1,2304]{3,2,1,0:T(1,128)S(1)} %bitcast.19) | data formatting | bytes 589824
  51.0 0.4 copy-done
  51.4 0.0 copy-start.4
  51.4 0.7 %copy.36 = f32[32,1,1,2304]{3,2,1,0:T(1,128)} copy(f32[32,1,1,2304]{3,2,1,0:T(1,128)S(1)} %bitcast.18) | data formatting | bytes 589824
  52.1 0.0 copy-done.4
  52.1 0.6 %copy.37 = f32[3,128]{1,0:T(4,128)} copy(f32[3,128]{1,0:T(4,128)S(1)} %copy-done.4) | data formatting | bytes 3072
Async XLA Ops:
  45.8 1.4 %copy-start.3 = (f32[64,128]{1,0:T(8,128)S(1)}, f32[64,128]{1,0:T(8,128)}, u32[]{:S(2)}) copy-start(f32[64,128]{1,0:T(8,128)} %get-tuple-element.36) | copy-start | bytes 98308
  47.2 0.8 %copy-start.2 = (f32[64,128]{1,0:T(8,128)S(1)}, f32[64,128]{1,0:T(8,128)}, u32[]{:S(2)}) copy-start(f32[64,128]{1,0:T(8,128)} %get-tuple-element.37) | copy-start | bytes 98308
  48.6 1.8 %copy-start.1 = (f32[576,128]{1,0:T(8,128)S(1)}, f32[576,128]{1,0:T(8,128)}, u32[]{:S(2)}) copy-start(f32[576,128]{1,0:T(8,128)} %get-tuple-element.18) | copy-start | bytes 884740
  50.3 1.1 %copy-start = (f32[576,128]{1,0:T(8,128)S(1)}, f32[576,128]{1,0:T(8,128)}, u32[]{:S(2)}) copy-start(f32[576,128]{1,0:T(8,128)} %get-tuple-element.19) | copy-start | bytes 884740
  51.4 0.7 %copy-start.4 = (f32[3,128]{1,0:T(4,128)S(1)}, f32[3,128]{1,0:T(4,128)}, u32[]{:S(2)}) copy-start(f32[3,128]{1,0:T(4,128)} %get-tuple-element.41) | copy-start | bytes 4612

commit v2 on v1

v2 whole, which is shorter than its diff:
```python
import functools

import jax
import jax.numpy as jnp
from jax import lax
from jax.experimental import pallas as pl
from jax.experimental.pallas import tpu as pltpu
from jax.sharding import PartitionSpec as P

MESH = pl.DeviceIdType.MESH
NA = 32
NB = 8
STEPS = 3
f32 = jnp.float32
i32 = jnp.int32


def lanes():
    return lax.broadcasted_iota(i32, (8, 128), 1)


def sublanes():
    return lax.broadcasted_iota(i32, (8, 128), 0)


def swap_blocks(x, sub, lg):
    for k in range(3):
        bs = (sub >> k) & 1
        bl = (lg >> k) & 1
        step = 16 << k
        down = pltpu.roll(pltpu.roll(x, 1 << k, 0), 128 - step, 1)
        up = pltpu.roll(pltpu.roll(x, 8 - (1 << k), 0), step, 1)
        x = jnp.where(bs == bl, x, jnp.where(bs == 1, down, up))
    return x


def lane_gather(x, idx):
    return jnp.take_along_axis(x, idx, axis=1)


def div(x, n):
    return (x * ((1 << 20) // n + 1)) >> 20


FINE = 48


def sources_of_cells():
    need = [set() for _ in range(18)]
    back = [set() for _ in range(18)]
    for p in range(FINE):
        for q in range(FINE):
            u, g = 3 * (p % 6) + q % 3, (p * FINE + q) // 128
            need[u].add(g)
            back[g].add(u)
    return [sorted(x) for x in need], [sorted(x) for x in back]


NEED, BACK = sources_of_cells()


def pick(table, ids):
    bits = [(ids & (1 << k)) != 0 for k in range(3)]
    for bit in bits:
        table = [jnp.where(bit, table[i + 1], table[i]) for i in range(0, len(table), 2)]
    return table[0]


def step_tables(eps, sig, ratio):
    loss = sig / (eps * ratio)
    return (1.0 - loss) / (1.0 + loss), 0.5 / (eps * (1.0 + loss))


def kernel(
    ez_in, hx_in, hy_in, ids_in, eps_in, sig_in, fez_in, fhx_in, fhy_in, fids_in, box_in, src_in, wave_in, rcv_in,
    ez_out, hx_out, hy_out, fez_out, fhx_out, fhy_out, tr_out,
    HE, IDS, PB, PEL, PER, E2, S1, R1, S2, R2, O1, RO1, O2, RO2, TS, TB, TS2, TG,
    FI, FD, FG, WE, WX, WY, IDX, SEL, TAB, CO, BOX, SRC, WAVE, RCV, EPS, SIG,
    in_sem, halo_sem, halo_send, send_sem, recv_sem, stage_sem,
):
    FE, FX, FY = fez_out, fhx_out, fhy_out
    grp = lax.axis_index("grp")
    a = lax.axis_index("gx")
    gy = lax.axis_index("gy")
    b = grp * 4 + gy

    def dev(na, nb):
        return (nb // 4, na, nb % 4)

    am, ap = lax.rem(a + NA - 1, NA), lax.rem(a + 1, NA)
    bm, bp = lax.rem(b + NB - 1, NB), lax.rem(b + 1, NB)

    loads = []
    for j, (source, dst) in enumerate((
        (ez_in, HE.at[0, pl.ds(8, 64), :]),
        (hx_in, HE.at[1, pl.ds(8, 64), :]),
        (hy_in, HE.at[2, pl.ds(8, 64), :]),
        (ids_in, IDS),
        (fids_in, FI),
        (fez_in, FE),
        (fhx_in, FX),
        (fhy_in, FY),
        (box_in, BOX),
        (eps_in, EPS),
        (sig_in, SIG),
        (rcv_in, RCV),
        (src_in, SRC),
        (wave_in, WAVE),
    )):
        copy = pltpu.make_async_copy(source, dst, in_sem.at[j])
        copy.start()
        loads.append(copy)

    barrier = pltpu.get_barrier_semaphore()

    def signal(na, nb):
        pl.semaphore_signal(barrier, inc=1, device_id=dev(na, nb), device_id_type=MESH)

    y, z = a // 8, lax.rem(a, 8)
    for na in (am, ap):
        for nb in (bm, b, bp):
            signal(na, nb)
    for d in range(1, NB):
        signal(a, lax.rem(b + d, NB))
    for d in range(1, 8):
        signal(y * 8 + lax.rem(z + d, 8), b)
    y_peers = [lax.rem(y + d, 4) * 8 + z for d in range(1, 4)]
    for n in y_peers:
        signal(n, b)

    lane = lanes()
    sub = sublanes()
    lg = lane >> 4

    for g in range(18):
        pos = lane + 128 * g
        p = div(pos, 48)
        q = pos - 48 * p
        pb, j = div(p, 6), div(q, 3)
        IDX[pl.ds(8 * g, 8), :] = 16 * pb + j
        SEL[pl.ds(8 * g, 8), :] = 3 * (p - 6 * pb) + (q - 3 * j)
    cell_pos = 288 * (lane >> 4) + 3 * (lane & 15)

    def flat_rows(tg, g):
        return pl.ds(tg * 144 + g, 8, stride=18)

    def cell_rows(tg, u):
        return pl.ds(pl.multiple_of(tg * 144 + 8 * u, 8), 8)

    def to_cells(src, put):
        def body(tg, carry):
            flat = [src[flat_rows(tg, g), :] for g in range(18)]
            for u in range(18):
                pos = cell_pos + (48 * (u // 3) + u % 3)
                idx, group = pos & 127, pos >> 7
                value = lane_gather(flat[NEED[u][0]], idx)
                for g in NEED[u][1:]:
                    value = jnp.where(group == g, lane_gather(flat[g], idx), value)
                put(tg, u, value)
            return carry

        lax.fori_loop(0, 4, body, 0)

    def put_in(dst):
        def put(tg, u, value):
            dst[cell_rows(tg, u), :] = value

        return put

    def from_cells(src, dst):
        def body(tg, carry):
            cells = [src[cell_rows(tg, u), :] for u in range(18)]
            for g in range(18):
                idx, group = IDX[pl.ds(8 * g, 8), :], SEL[pl.ds(8 * g, 8), :]
                value = lane_gather(cells[BACK[g][0]], idx)
                for u in BACK[g][1:]:
                    value = jnp.where(group == u, lane_gather(cells[u], idx), value)
                dst[flat_rows(tg, g), :] = value
            return carry

        lax.fori_loop(0, 4, body, 0)

    for copy in loads[:4] + loads[8:]:
        copy.wait()
    HE[3, pl.ds(8, 64), :] = IDS[...].astype(f32)

    for v in range(8):
        ci, h = v // 2, v % 2
        for k in range(4):
            x = HE[k, pl.ds(8 + 16 * ci + h, 8, stride=2), :]
            S1[pl.ds(ci * 128 + 2 * k + h, 8, stride=16), :] = swap_blocks(x, sub, lg)
    row32 = lax.broadcasted_iota(i32, (32, 32), 0)
    col32 = lax.broadcasted_iota(i32, (32, 32), 1)
    lane32 = lax.broadcasted_iota(i32, (32, 128), 1)
    box_rows = jnp.zeros((32, 128), f32)
    for k in range(4):
        one = jnp.broadcast_to(BOX[pl.ds(k, 1), :], (32, 32)).astype(f32)
        value = jnp.sum(jnp.where(row32 == col32, one, 0.0), axis=1, keepdims=True)
        box_rows = jnp.where(lane32 == k, value, box_rows)
    S1[pl.ds(8, 32, stride=16), :] = box_rows

    lane64 = lax.broadcasted_iota(i32, (64, 128), 1)
    packed = jnp.zeros((64, 128), f32)
    for k in range(4):
        near = (lane64 - 8 * k) & 127
        x = HE[k, pl.ds(8, 64), :]
        packed = jnp.where((near < 3) | (near >= 125), pltpu.roll(x, 8 * k, 1) if k else x, packed)
    PB[...] = packed

    TAB[pl.ds(0, 8), :] = jnp.ones((8, 128), f32)
    TAB[pl.ds(8, 8), :] = jnp.zeros((8, 128), f32)
    TAB[pl.ds(0, 8), pl.ds(0, 8)] = jnp.broadcast_to(EPS[...], (8, 8))
    TAB[pl.ds(8, 8), pl.ds(0, 8)] = jnp.broadcast_to(SIG[...], (8, 8))
    eps, sig = TAB[pl.ds(0, 8), :], TAB[pl.ds(8, 8), :]
    for j, table in enumerate(step_tables(eps, sig, 1.0) + step_tables(eps, sig, 3.0)):
        for k in range(8):
            TAB[pl.ds(16 + 64 * j + 8 * k, 8), :] = jnp.broadcast_to(table[:, k : k + 1], (8, 128))

    def table(j):
        return [TAB[pl.ds(16 + 64 * j + 8 * k, 8), :] for k in range(8)]

    damp1, gain1, damp3, gain3 = (functools.partial(table, j) for j in range(4))


    def put_coef(tg, u, ids):
        FD[cell_rows(tg, u), :] = pick(damp3(), ids)
        FG[cell_rows(tg, u), :] = pick(gain3(), ids)

    pl.semaphore_wait(barrier, 6 + (NB - 1) + 7 + 3)
    for n in y_peers:
        pl.semaphore_signal(stage_sem, inc=1, device_id=dev(n, b), device_id_type=MESH)

    halos = []

    def halo(j, src, dst, na, nb):
        copy = pltpu.make_async_remote_copy(
            src_ref=src, dst_ref=dst, send_sem=halo_send.at[j], recv_sem=halo_sem.at[j],
            device_id=dev(na, nb), device_id_type=MESH,
        )
        copy.start()
        halos.append(copy)

    halo(0, HE.at[:, pl.ds(64, 8), :], HE.at[:, pl.ds(0, 8), :], ap, b)
    halo(1, HE.at[:, pl.ds(8, 8), :], HE.at[:, pl.ds(72, 8), :], am, b)
    halo(2, PB, PEL.at[pl.ds(8, 64), :], a, bp)
    halo(3, PB, PER.at[pl.ds(8, 64), :], a, bm)
    halo(4, PB.at[pl.ds(56, 8), :], PEL.at[pl.ds(0, 8), :], ap, bp)
    halo(5, PB.at[pl.ds(56, 8), :], PER.at[pl.ds(0, 8), :], ap, bm)
    halo(6, PB.at[pl.ds(0, 8), :], PEL.at[pl.ds(72, 8), :], am, bp)
    halo(7, PB.at[pl.ds(0, 8), :], PER.at[pl.ds(72, 8), :], am, bm)

    def ring(d, size):
        return min(d, size - d)

    offsets = sorted(
        ((dy, dz) for dy in range(4) for dz in range(8) if dy or dz), key=lambda o: -(ring(o[0], 4) + ring(o[1], 8))
    )
    peers = [lax.rem(a // 8 + dy, 4) * 8 + lax.rem(lax.rem(a, 8) + dz, 8) for dy, dz in offsets]

    def exchange(j, src, dst, slot, rows, same=False):
        own = pl.multiple_of(a * slot, slot)
        for n in peers:
            pltpu.make_async_remote_copy(
                src_ref=src.at[pl.ds(0 if same else pl.multiple_of(n * slot, slot), rows), :],
                dst_ref=dst.at[pl.ds(own, rows), :],
                send_sem=send_sem.at[j], recv_sem=recv_sem.at[j],
                device_id=dev(n, b), device_id_type=MESH,
            ).start()
        dst[pl.ds(own, rows), :] = src[pl.ds(0 if same else own, rows), :]

    def received(j, buf, rows):
        total = (NA - 1) * rows
        return pltpu.make_async_copy(buf.at[pl.ds(0, total), :], buf.at[pl.ds(0, total), :], recv_sem.at[j])

    def sent(j, buf, rows):
        total = (NA - 1) * rows
        return pltpu.make_async_copy(buf.at[pl.ds(0, total), :], buf.at[pl.ds(0, total), :], send_sem.at[j])

    loads[4].wait()
    to_cells(FI, put_coef)
    pl.semaphore_wait(stage_sem, 3)
    exchange(0, S1, R1, 16, 9)

    loads[5].wait()
    to_cells(FE, put_in(WE))

    for copy in halos:
        copy.wait()
    lane80 = lax.broadcasted_iota(i32, (80, 128), 1)
    row80 = lax.broadcasted_iota(i32, (80, 128), 0)
    row_g = row80 + (a * 64 - 8)
    col_m = lane80 + b * 128
    col_s = jnp.where(lane80 < 64, col_m + 128, col_m - 128)
    row_ok = (row_g >= 0) & (row_g < NA * 64)
    ok_m = jnp.where(row_ok, 1.0, 0.0)
    ok_s = jnp.where(row_ok & (col_s >= 0) & (col_s < NB * 128), 1.0, 0.0)

    def sides(k):
        left, right = PEL[...], PER[...]
        if k:
            left, right = pltpu.roll(left, 128 - 8 * k, 1), pltpu.roll(right, 128 - 8 * k, 1)
        return jnp.where(lane80 >= 125, left, jnp.where(lane80 < 3, right, 0.0))

    pair_ez, pair_hx, pair_hy = ((HE[k] * ok_m, sides(k) * ok_s) for k in range(3))

    def coef80(table, ids, ok):
        parts = [pick(table, ids[8 * r : 8 * r + 8, :].astype(i32)) for r in range(10)]
        return jnp.concatenate(parts, axis=0) * ok

    ids_m, ids_s = HE[3], sides(3)
    pair_damp = (coef80(damp1(), ids_m, ok_m), coef80(damp1(), ids_s, ok_s))
    pair_gain = (coef80(gain1(), ids_m, ok_m), coef80(gain1(), ids_s, ok_s))

    def right_of(x):
        m, s = pltpu.roll(x[0], 127, 1), pltpu.roll(x[1], 127, 1)
        return jnp.where(lane80 < 127, m, s), jnp.where(lane80 < 127, s, m)

    def left_of(x):
        m, s = pltpu.roll(x[0], 1, 1), pltpu.roll(x[1], 1, 1)
        return jnp.where(lane80 >= 1, m, s), jnp.where(lane80 >= 1, s, m)

    def below(x):
        return pltpu.roll(x[0], 79, 0), pltpu.roll(x[1], 79, 0)

    def above(x):
        return pltpu.roll(x[0], 1, 0), pltpu.roll(x[1], 1, 0)

    def both(fn, *pairs):
        return tuple(fn(*(p[i] for p in pairs)) for i in range(2))

    src_i = [SRC[0, k] >> 10 for k in range(4)]
    src_j = [SRC[0, k] & 1023 for k in range(4)]

    def h_step(ez, hx, hy):
        hx = both(lambda h, e, r, k: (h - 0.5 * (r - e)) * k, hx, ez, right_of(ez), (ok_m, ok_s))
        hy = both(lambda h, e, r, k: (h + 0.5 * (r - e)) * k, hy, ez, below(ez), (ok_m, ok_s))
        return hx, hy

    for n in range(2):
        pair_hx, pair_hy = h_step(pair_ez, pair_hx, pair_hy)
        drive = []
        for col in (col_m, col_s):
            total = jnp.zeros((80, 128), f32)
            for k in range(4):
                total = total + jnp.where((row_g == src_i[k]) & (col == src_j[k]), WAVE[n, k], 0.0)
            drive.append(total)
        pair_ez = both(
            lambda d, e, g, hy, hu, hx, hl, s: d * e + g * ((hy - hu) - (hx - hl)) + s,
            pair_damp, pair_ez, pair_gain, pair_hy, above(pair_hy), pair_hx, left_of(pair_hx), tuple(drive),
        )
        E2[n] = pair_ez[0][8:72, :]
    pair_hx, pair_hy = h_step(pair_ez, pair_hx, pair_hy)
    E2[2] = jnp.where((row80 & 15) == 8, above(pair_hy)[0], pair_hy[0])[8:72, :]
    E2[3] = jnp.where((lane80 & 15) == 0, left_of(pair_hx)[0], pair_hx[0])[8:72, :]

    e4, t16 = (lane >> 4) & 3, lane & 15
    frame_idx = jnp.where(
        e4 == 0, t16,
        jnp.where(e4 == 1, 112 + t16, jnp.where(e4 == 2, 16 * (t16 >> 1), 16 * (t16 >> 1) + 15)),
    )
    from_h1 = jnp.where(e4 == 0, 0, jnp.where(e4 == 1, 1, t16 & 1)) == 1

    for ci in range(4):
        got = []
        for k in range(4):
            halves = []
            for h in range(2):
                x = E2[k, pl.ds(16 * ci + h, 8, stride=2), :]
                halves.append(lane_gather(swap_blocks(x, sub, lg), frame_idx))
            got.append(jnp.where(from_h1, halves[1], halves[0]))
        S2[pl.ds(ci * 64, 8, stride=8), :] = jnp.where(lane < 64, got[0], got[1])
        S2[pl.ds(ci * 64 + 1, 8, stride=8), :] = jnp.where((lane & 63) < 32, got[2], got[3])

    exchange(1, S2, R2, 8, 2)

    loads[6].wait()
    to_cells(FX, put_in(WX))
    loads[7].wait()
    to_cells(FY, put_in(WY))
    received(0, R1, 9).wait()

    def from1(k):
        return tuple(R1[pl.ds(2 * k + h, 32, stride=16), :] for h in range(2))

    ez, hx, hy, ids_c = (from1(k) for k in range(4))

    def coef32(table, ids):
        parts = [pick(table, ids[8 * r : 8 * r + 8, :].astype(i32)) for r in range(4)]
        return jnp.concatenate(parts, axis=0)

    damp = tuple(coef32(damp1(), x) for x in ids_c)
    gain = tuple(coef32(gain1(), x) for x in ids_c)
    rows_in = tuple(2 * (lane32 >> 4) + h for h in range(2))
    col_in = lane32 & 15
    boxes = R1[pl.ds(8, 32, stride=16), :]
    lo_i, lo_j, n_i, n_j = (jnp.broadcast_to(boxes[:, k : k + 1], (32, 128)).astype(i32) for k in range(4))
    mid = tuple((r > lo_i) & (r < lo_i + n_i - 1) & (col_in > lo_j) & (col_in < lo_j + n_j - 1) for r in rows_in)
    inbox = tuple((r >= lo_i) & (r < lo_i + n_i) & (col_in >= lo_j) & (col_in < lo_j + n_j) for r in rows_in)
    f_mid = tuple(jnp.where(m, 1.0, 0.0) for m in mid)
    f_in = tuple(jnp.where(m, 1.0, 0.0) for m in inbox)
    f_rim = both(lambda x, y: x - y, f_in, f_mid)
    for h in range(2):
        CO[0, pl.ds(32 * h, 32), :] = 0.5 * f_in[h]
        CO[4, pl.ds(32 * h, 32), :] = f_mid[h]

    def co_rows(tg, h):
        return pl.ds(pl.multiple_of(32 * h + 8 * tg, 8), 8)

    def prepare(tg, carry):
        halves = [(2.0 * CO[0, co_rows(tg, h), :], CO[4, co_rows(tg, h), :]) for h in range(2)]
        for u in range(18):
            box, middle = halves[u // 9]
            rows = cell_rows(tg, u)
            WX[rows, :] = WX[rows, :] * box
            WY[rows, :] = WY[rows, :] * box
            FD[rows, :] = FD[rows, :] * middle
            FG[rows, :] = FG[rows, :] * middle
        return carry

    lax.fori_loop(0, 4, prepare, 0)

    def substep(k, carry):
        m, tg = k // 4, lax.rem(k, 4)
        half_box = [CO[0, co_rows(tg, h), :] for h in range(2)]
        rim = [CO[1 + m, co_rows(tg, h), :] for h in range(2)]
        e = [WE[cell_rows(tg, u), :] for u in range(18)]
        x, y = [None] * 18, [None] * 18

        def magnetic(p):
            for u in range(3 * p, 3 * p + 3):
                c = half_box[u // 9]
                after = e[u + 1] if u % 3 < 2 else pltpu.roll(e[u - 2], 127, 1)
                under = e[u + 3] if u < 15 else pltpu.roll(e[u - 15], 112, 1)
                x[u] = WX[cell_rows(tg, u), :] - c * (after - e[u])
                y[u] = WY[cell_rows(tg, u), :] + c * (under - e[u])
                WX[cell_rows(tg, u), :] = x[u]
                WY[cell_rows(tg, u), :] = y[u]

        def electric(p):
            for u in range(3 * p, 3 * p + 3):
                before = x[u - 1] if u % 3 else pltpu.roll(x[u + 2], 1, 1)
                over = y[u - 3] if u >= 3 else pltpu.roll(y[u + 15], 16, 1)
                curl = (y[u] - over) - (x[u] - before)
                WE[cell_rows(tg, u), :] = (
                    FD[cell_rows(tg, u), :] * e[u] + FG[cell_rows(tg, u), :] * curl + rim[u // 9]
                )

        magnetic(5)
        magnetic(0)
        for p in range(1, 5):
            magnetic(p)
            electric(p - 1)
        electric(4)
        electric(5)
        return carry

    def means(tg, carry):
        for h in range(2):
            part = [WE[cell_rows(tg, u), :] for u in range(9 * h, 9 * h + 9)]
            total = ((part[0] + part[1]) + (part[2] + part[3])) + ((part[4] + part[5]) + (part[6] + part[7])) + part[8]
            CO[5, co_rows(tg, h), :] = total * (1.0 / 9.0)
        return carry

    edge_col = (col_in == 0) | (col_in == 15)
    frame = (edge_col | (rows_in[0] == 0), edge_col | (rows_in[1] == 15))
    tile32 = lax.broadcasted_iota(i32, (32, 128), 0)
    my_ci, my_cj = a // 8, lax.rem(a, 8)
    src_tile, src_cell = [], []
    for k in range(4):
        i, j = src_i[k], src_j[k]
        here = ((i & 63) >> 4 == my_ci) & ((j & 127) >> 4 == my_cj) & (j >> 7 == b)
        src_tile.append(jnp.where(here, i >> 6, -1))
        src_cell.append((i & 1) * 128 + ((i & 15) >> 1) * 16 + (j & 15))
    rcv = jnp.broadcast_to(RCV[...], (8, 128))
    ri, rj = rcv >> 10, rcv & 1023
    r_here = (((ri & 63) >> 4) == my_ci) & (((rj & 127) >> 4) == my_cj) & ((rj >> 7) == b)
    r_tile = jnp.where(r_here, ri >> 6, -1)
    r_idx, r_half = ((ri & 15) >> 1) * 16 + (rj & 15), ri & 1

    def c_right(x):
        return tuple(pltpu.roll(v, 127, 1) for v in x)

    def c_left(x):
        return tuple(pltpu.roll(v, 1, 1) for v in x)

    def c_below(x):
        return x[1], pltpu.roll(x[0], 112, 1)

    def c_above(x):
        return pltpu.roll(x[1], 16, 1), x[0]

    for n in range(STEPS):
        hx = both(lambda h, e, r: h - 0.5 * (r - e), hx, ez, c_right(ez))
        hy = both(lambda h, e, r: h + 0.5 * (r - e), hy, ez, c_below(ez))
        hx_left, hy_up = c_left(hx), c_above(hy)
        if n == 2:
            edge = R2[pl.ds(1, 32, stride=8), :]

            def spread(idx):
                parts = [lane_gather(edge[8 * r : 8 * r + 8, :], idx) for r in range(4)]
                return jnp.concatenate(parts, axis=0)

            w1 = tuple(spread(t16 + 16 * h) for h in range(2))
            w2 = tuple(spread(jnp.where(t16 == 15, 48, 32) + 2 * (lane >> 4) + h) for h in range(2))
            hy = (hy[0], jnp.where(rows_in[1] == 15, w1[1], hy[1]))
            hx = tuple(jnp.where(col_in == 15, w2[h], hx[h]) for h in range(2))
            hy_up = (jnp.where(rows_in[0] == 0, w1[0], hy_up[0]), hy_up[1])
            hx_left = tuple(jnp.where(col_in == 0, w2[h], hx_left[h]) for h in range(2))
            for h in range(2):
                O1[pl.ds(h, 32, stride=8), :] = hx[h]
                O1[pl.ds(2 + h, 32, stride=8), :] = hy[h]
            exchange(2, O1, RO1, 8, 4)
        drive = []
        for h in range(2):
            total = jnp.zeros((32, 128), f32)
            for k in range(4):
                total = total + jnp.where(
                    (tile32 == src_tile[k]) & (lane32 + 128 * h == src_cell[k]), WAVE[n, k], 0.0
                )
            drive.append(total)
        new = both(
            lambda d, e, g, y, yu, x, xl, s: d * e + g * ((y - yu) - (x - xl)) + s,
            damp, ez, gain, hy, hy_up, hx, hx_left, tuple(drive),
        )
        for m in range(3):
            share = (m + 1) / 3.0
            for h in range(2):
                CO[1 + m, pl.ds(32 * h, 32), :] = f_rim[h] * ((1.0 - share) * ez[h] + share * new[h])
        lax.fori_loop(0, 12, substep, 0)
        lax.fori_loop(0, 4, means, 0)
        if n == 0:
            received(1, R2, 2).wait()
        if n < 2:
            rim = R2[pl.ds(0, 32, stride=8), :]
            out = []
            for h in range(2):
                r = 2 * (lane >> 4) + h
                slot = jnp.where(
                    r == 0, t16, jnp.where(r == 15, 16 + t16, jnp.where(t16 == 0, 32 + r, 48 + r))
                )
                slot = (slot & 63) + 64 * n
                parts = [lane_gather(rim[8 * q : 8 * q + 8, :], slot) for q in range(4)]
                out.append(jnp.where(frame[h], jnp.concatenate(parts, axis=0), new[h]))
            new = tuple(out)
        ez = both(lambda m, x, y: jnp.where(m, x, y), mid, (CO[5, pl.ds(0, 32), :], CO[5, pl.ds(32, 32), :]), new)
        picked = jnp.zeros((8, 128), f32)
        for h in range(2):
            for q in range(4):
                got = lane_gather(ez[h][8 * q : 8 * q + 8, :], r_idx)
                picked = picked + jnp.where((r_tile == sub + 8 * q) & (r_half == h), got, 0.0)
        TS[pl.ds(n, 1), :] = jnp.sum(picked, axis=0, keepdims=True)

    for d in range(1, NB):
        n = lax.rem(b + d, NB)
        pltpu.make_async_remote_copy(
            src_ref=TS.at[pl.ds(0, 3), :],
            dst_ref=TB.at[pl.ds(pl.multiple_of(8 * b, 8), 3), :],
            send_sem=send_sem.at[4], recv_sem=recv_sem.at[4],
            device_id=dev(a, n), device_id_type=MESH,
        ).start()
    TB[pl.ds(pl.multiple_of(8 * b, 8), 3), :] = TS[pl.ds(0, 3), :]

    for h in range(2):
        O2[pl.ds(h, 32, stride=8), :] = ez[h]
    exchange(3, O2, RO2, 8, 2)

    from_cells(WE, FE)
    from_cells(WX, FX)
    seven = (NB - 1) * 3
    pltpu.make_async_copy(TB.at[pl.ds(0, seven), :], TB.at[pl.ds(0, seven), :], recv_sem.at[4]).wait()
    for n in range(STEPS):
        TS2[pl.ds(n, 1), :] = jnp.sum(TB[pl.ds(n, 8, stride=8), :], axis=0, keepdims=True)
    exchange(5, TS2, TG, 8, 3, same=True)

    from_cells(WY, FY)
    received(2, RO1, 4).wait()

    def unpack(src, first, dst):
        for ci in range(4):
            for h in range(2):
                x = src[pl.ds(ci * 64 + first + h, 8, stride=8), :]
                dst[pl.ds(16 * ci + h, 8, stride=2), :] = swap_blocks(x, sub, lg)

    unpack(RO1, 0, hx_out)
    unpack(RO1, 2, hy_out)
    received(3, RO2, 2).wait()
    unpack(RO2, 0, ez_out)
    received(5, TG, 3).wait()
    for n in range(STEPS):
        tr_out[pl.ds(n, 1), :] = jnp.sum(TG[pl.ds(n, 32, stride=8), :], axis=0, keepdims=True)

    for j, buf, rows in ((0, S1, 9), (1, S2, 2), (2, O1, 4), (3, O2, 2), (5, TG, 3)):
        sent(j, buf, rows).wait()
    pltpu.make_async_copy(TB.at[pl.ds(0, seven), :], TB.at[pl.ds(0, seven), :], send_sem.at[4]).wait()


def finish(*refs):
    sources, outs, sems = refs[:7], refs[7:14], refs[14]
    copies = [pltpu.make_async_copy(x, y, sems.at[j]) for j, (x, y) in enumerate(zip(sources, outs))]
    for copy in copies:
        copy.start()
    for copy in copies:
        copy.wait()


def shards(
    coarse_ez, coarse_hx, coarse_hy, coarse_ids, mat_eps, mat_sig,
    fine_ez, fine_hx, fine_hy, fine_ids, boxes, src_cells, src_wave, rcv_cells,
):
    fine_shape = fine_ez.shape
    flat = (576, 128)
    anywhere = pl.BlockSpec(memory_space=pl.ANY)
    vmem = pl.BlockSpec(memory_space=pltpu.VMEM)
    shapes = ((64, 128),) * 3 + (flat,) * 3 + ((3, 128),)

    def v(*shape, dtype=f32):
        return pltpu.VMEM(shape, dtype)

    def dma(n):
        return pltpu.SemaphoreType.DMA((n,))

    outs = pl.pallas_call(
        kernel,
        name="nested",
        out_shape=tuple(pltpu.VMEM(shape, f32) for shape in shapes),
        in_specs=[anywhere] * 14,
        out_specs=(vmem,) * 7,
        scratch_shapes=[
            v(4, 80, 128), v(64, 128, dtype=i32), v(64, 128), v(80, 128), v(80, 128), v(4, 64, 128),
            v(512, 128), v(512, 128), v(256, 128), v(256, 128),
            v(256, 128), v(256, 128), v(256, 128), v(256, 128),
            v(8, 128), v(64, 128), v(8, 128), v(256, 128),
            v(576, 128, dtype=i32), v(584, 128), v(584, 128),
            v(584, 128), v(584, 128), v(584, 128),
            v(144, 128, dtype=i32), v(144, 128, dtype=i32), v(272, 128), v(6, 64, 128),
            v(4, 32, dtype=i32), pltpu.SMEM((1, 4), i32), pltpu.SMEM((3, 4), f32),
            v(1, 128, dtype=i32), v(1, 8), v(1, 8),
            dma(14), dma(8), dma(8), dma(6), dma(6), pltpu.SemaphoreType.REGULAR,
        ],
        compiler_params=pltpu.CompilerParams(collective_id=0, has_side_effects=True),
    )(
        coarse_ez, coarse_hx, coarse_hy, coarse_ids,
        mat_eps.reshape(1, 8), mat_sig.reshape(1, 8),
        fine_ez.reshape(flat), fine_hx.reshape(flat), fine_hy.reshape(flat), fine_ids.reshape(flat),
        boxes.reshape(32, 4).T, src_cells.reshape(1, 4), src_wave, rcv_cells.reshape(1, 128),
    )
    outs = pl.pallas_call(
        finish,
        name="finish",
        out_shape=tuple(jax.ShapeDtypeStruct(shape, f32) for shape in shapes),
        in_specs=[vmem] * 7,
        out_specs=(anywhere,) * 7,
        scratch_shapes=[dma(7)],
    )(*(pltpu.with_memory_space_constraint(x, pltpu.VMEM) for x in outs))
    return tuple(outs[:3]) + tuple(x.reshape(fine_shape) for x in outs[3:6]) + (outs[6],)


def solution(mesh):
    coarse = P("gx", ("grp", "gy"))
    tiles = P(None, ("grp", "gy"), "gx", None)
    in_specs = (
        coarse, coarse, coarse, coarse, P(), P(), tiles, tiles, tiles, tiles,
        P("gx", ("grp", "gy"), None, None), P(), P(), P(),
    )
    out_specs = (coarse, coarse, coarse, tiles, tiles, tiles, P())
    return jax.shard_map(shards, mesh=mesh, in_specs=in_specs, out_specs=out_specs, check_vma=False)
```

time: 53 us -> 38 us (0.72)
  Pallas kernels: 45.1 us -> 37.2 us
  local copies, waits for them, and re-layouts: 6.88 us -> 0 us
    pallas_call x1 -> x2, Pallas kernels: 45.1 us -> 37.2 us  [the longest x1 36.2 us: shards(): pl.pallas_call(kernel, name='nested', out_shape=tuple((pltpu.VMEM(shape,...]
    unnamed x17 -> x0, local copies, waits for them, and re-layouts: 6.88 us -> none
where the time goes in v2:
time: 38 us; the launch traced here: 37.9 us
  Pallas kernels  37.2 us (98%)
  between operations  0.65 us (2%)
    pallas_call x1, Pallas kernels, shards(): pl.pallas_call(kernel, name='nested', out_shape=tuple((pltpu.VMEM(shape,...  36.2 us
    pallas_call x1, Pallas kernels, shards(): pl.pallas_call(finish, name='finish', out_shape=tuple((jax.ShapeDtypeStru...  1.01 us

profile of v2, /device:TPU:1, one launch (start us, length us, event | category | flops | bytes accessed | tf_op | source)
XLA Modules:
  0.0 37.9 jit_solution(7026118625827407327)
XLA Ops:
  0.6 36.2 %nested.1 = (f32[64,128]{1,0:T(8,128)S(1)}, f32[64,128]{1,0:T(8,128)S(1)}, f32[64,128]{1,0:T(8,128)S(1)}, f32[576,128]{1,0:T(8,128)S(1)}, f32[576,128]{1,0:T(8,1...) custom-call(f32[64,128]{1,0:T(8,128)} %ez_in.1, f32[64,128]{1,0:T(8,128)} %hx_in.1, f32[64,128]{1,0:T(8,128)} %hy_in.1, ...), custom_call_target="tpu_custom_call" | custom-call | tf_op jit(solution)/shard_map/nested/pallas_call | solution.py:622
  36.9 1.0 %finish.1 = (f32[64,128]{1,0:T(8,128)}, f32[64,128]{1,0:T(8,128)}, f32[64,128]{1,0:T(8,128)}, f32[576,128]{1,0:T(8,128)}, f32[576,128]{1,0:T(8,128)}, /*index=5*/f32[576,128]{1,0:T(8,128)}, f32[3,128]{1,0:T(4,128)}) custom-call(f32[64,128]{1,0:T(8,128)S(1)} %get-tuple-element.21.refs_0_, f32[64,128]{1,0:T(8,128)S(1)} %get-tuple-element.22.refs_1_, ...), custom_call_target="tpu_custom_call" | custom-call | tf_op jit(solution)/shard_map/finish/pallas_call | solution.py:647

commit v3 on v2

--- a/solution.py
+++ b/solution.py
@@ -74,9 +74,9 @@
 def kernel(
     ez_in, hx_in, hy_in, ids_in, eps_in, sig_in, fez_in, fhx_in, fhy_in, fids_in, box_in, src_in, wave_in, rcv_in,
     ez_out, hx_out, hy_out, fez_out, fhx_out, fhy_out, tr_out,
-    HE, IDS, PB, PEL, PER, E2, S1, R1, S2, R2, O1, RO1, O2, RO2, TS, TB, TS2, TG,
+    HE, DG, IDS, PB, PEL, PER, E2, S1, R1, S2, R2, O1, RO1, TS, TB, TS2, TG,
     FI, FD, FG, WE, WX, WY, IDX, SEL, TAB, CO, BOX, SRC, WAVE, RCV, EPS, SIG,
-    in_sem, halo_sem, halo_send, send_sem, recv_sem, stage_sem,
+    MANY, in_sem, halo_sem, send_sem, recv_sem, stage_sem,
 ):
     FE, FX, FY = fez_out, fhx_out, fhy_out
     grp = lax.axis_index("grp")
@@ -89,6 +89,9 @@
 
     am, ap = lax.rem(a + NA - 1, NA), lax.rem(a + 1, NA)
     bm, bp = lax.rem(b + NB - 1, NB), lax.rem(b + 1, NB)
+
+    def bytes_of(rows, sem):
+        return pltpu.make_async_copy(MANY.at[pl.ds(0, rows), :], MANY.at[pl.ds(0, rows), :], sem)
 
     loads = []
     for j, (source, dst) in enumerate((
@@ -107,7 +110,7 @@
         (src_in, SRC),
         (wave_in, WAVE),
     )):
-        copy = pltpu.make_async_copy(source, dst, in_sem.at[j])
+        copy = pltpu.make_async_copy(source, dst, in_sem.at[min(j // 4, 2) + max(j - 8, 0)])
         copy.start()
         loads.append(copy)
 
@@ -144,11 +147,22 @@
     def flat_rows(tg, g):
         return pl.ds(tg * 144 + g, 8, stride=18)
 
+    def aligned(start, size):
+        return pl.ds(start if isinstance(start, int) else pl.multiple_of(start, 8), size)
+
     def cell_rows(tg, u):
-        return pl.ds(pl.multiple_of(tg * 144 + 8 * u, 8), 8)
+        return aligned(tg * 144 + 8 * u, 8)
+
+    def each_pair(body):
+        def pair(half, carry):
+            for k in range(2):
+                body(2 * half + k)
+            return carry
+
+        lax.fori_loop(0, 2, pair, 0)
 
     def to_cells(src, put):
-        def body(tg, carry):
+        def body(tg):
             flat = [src[flat_rows(tg, g), :] for g in range(18)]
             for u in range(18):
                 pos = cell_pos + (48 * (u // 3) + u % 3)
@@ -157,9 +171,8 @@
                 for g in NEED[u][1:]:
                     value = jnp.where(group == g, lane_gather(flat[g], idx), value)
                 put(tg, u, value)
-            return carry
-
-        lax.fori_loop(0, 4, body, 0)
+
+        each_pair(body)
 
     def put_in(dst):
         def put(tg, u, value):
@@ -168,7 +181,7 @@
         return put
 
     def from_cells(src, dst):
-        def body(tg, carry):
+        def body(tg):
             cells = [src[cell_rows(tg, u), :] for u in range(18)]
             for g in range(18):
                 idx, group = IDX[pl.ds(8 * g, 8), :], SEL[pl.ds(8 * g, 8), :]
@@ -176,11 +189,11 @@
                 for u in BACK[g][1:]:
                     value = jnp.where(group == u, lane_gather(cells[u], idx), value)
                 dst[flat_rows(tg, g), :] = value
-            return carry
-
-        lax.fori_loop(0, 4, body, 0)
-
-    for copy in loads[:4] + loads[8:]:
+
+        each_pair(body)
+
+    bytes_of(4 * 64, in_sem.at[0]).wait()
+    for copy in loads[8:]:
         copy.wait()
     HE[3, pl.ds(8, 64), :] = IDS[...].astype(f32)
 
@@ -230,24 +243,21 @@
     for n in y_peers:
         pl.semaphore_signal(stage_sem, inc=1, device_id=dev(n, b), device_id_type=MESH)
 
-    halos = []
-
-    def halo(j, src, dst, na, nb):
+    def halo(src, dst, na, nb):
         copy = pltpu.make_async_remote_copy(
-            src_ref=src, dst_ref=dst, send_sem=halo_send.at[j], recv_sem=halo_sem.at[j],
+            src_ref=src, dst_ref=dst, send_sem=send_sem, recv_sem=halo_sem,
             device_id=dev(na, nb), device_id_type=MESH,
         )
         copy.start()
-        halos.append(copy)
-
-    halo(0, HE.at[:, pl.ds(64, 8), :], HE.at[:, pl.ds(0, 8), :], ap, b)
-    halo(1, HE.at[:, pl.ds(8, 8), :], HE.at[:, pl.ds(72, 8), :], am, b)
-    halo(2, PB, PEL.at[pl.ds(8, 64), :], a, bp)
-    halo(3, PB, PER.at[pl.ds(8, 64), :], a, bm)
-    halo(4, PB.at[pl.ds(56, 8), :], PEL.at[pl.ds(0, 8), :], ap, bp)
-    halo(5, PB.at[pl.ds(56, 8), :], PER.at[pl.ds(0, 8), :], ap, bm)
-    halo(6, PB.at[pl.ds(0, 8), :], PEL.at[pl.ds(72, 8), :], am, bp)
-    halo(7, PB.at[pl.ds(0, 8), :], PER.at[pl.ds(72, 8), :], am, bm)
+
+    halo(HE.at[:, pl.ds(64, 8), :], HE.at[:, pl.ds(0, 8), :], ap, b)
+    halo(HE.at[:, pl.ds(8, 8), :], HE.at[:, pl.ds(72, 8), :], am, b)
+    halo(PB, PEL.at[pl.ds(8, 64), :], a, bp)
+    halo(PB, PER.at[pl.ds(8, 64), :], a, bm)
+    halo(PB.at[pl.ds(56, 8), :], PEL.at[pl.ds(0, 8), :], ap, bp)
+    halo(PB.at[pl.ds(56, 8), :], PER.at[pl.ds(0, 8), :], ap, bm)
+    halo(PB.at[pl.ds(0, 8), :], PEL.at[pl.ds(72, 8), :], am, bp)
+    halo(PB.at[pl.ds(0, 8), :], PER.at[pl.ds(72, 8), :], am, bm)
 
     def ring(d, size):
         return min(d, size - d)
@@ -263,29 +273,28 @@
             pltpu.make_async_remote_copy(
                 src_ref=src.at[pl.ds(0 if same else pl.multiple_of(n * slot, slot), rows), :],
                 dst_ref=dst.at[pl.ds(own, rows), :],
-                send_sem=send_sem.at[j], recv_sem=recv_sem.at[j],
+                send_sem=send_sem, recv_sem=recv_sem.at[j],
                 device_id=dev(n, b), device_id_type=MESH,
             ).start()
         dst[pl.ds(own, rows), :] = src[pl.ds(0 if same else own, rows), :]
 
-    def received(j, buf, rows):
-        total = (NA - 1) * rows
-        return pltpu.make_async_copy(buf.at[pl.ds(0, total), :], buf.at[pl.ds(0, total), :], recv_sem.at[j])
-
-    def sent(j, buf, rows):
-        total = (NA - 1) * rows
-        return pltpu.make_async_copy(buf.at[pl.ds(0, total), :], buf.at[pl.ds(0, total), :], send_sem.at[j])
-
-    loads[4].wait()
+    def received(j, rows):
+        return bytes_of((NA - 1) * rows, recv_sem.at[j])
+
+    bytes_of(4 * 576, in_sem.at[1]).wait()
     to_cells(FI, put_coef)
     pl.semaphore_wait(stage_sem, 3)
     exchange(0, S1, R1, 16, 9)
 
-    loads[5].wait()
-    to_cells(FE, put_in(WE))
-
-    for copy in halos:
-        copy.wait()
+    def coef_rows(ids):
+        ids = ids.astype(i32)
+        return pick(damp1(), ids), pick(gain1(), ids)
+
+    for r in range(1, 9):
+        DG[0, pl.ds(8 * r, 8), :], DG[1, pl.ds(8 * r, 8), :] = coef_rows(HE[3, pl.ds(8 * r, 8), :])
+    bytes_of(2 * 32 + 2 * 64 + 4 * 8, halo_sem).wait()
+    for r in (0, 9):
+        DG[0, pl.ds(8 * r, 8), :], DG[1, pl.ds(8 * r, 8), :] = coef_rows(HE[3, pl.ds(8 * r, 8), :])
     lane80 = lax.broadcasted_iota(i32, (80, 128), 1)
     row80 = lax.broadcasted_iota(i32, (80, 128), 0)
     row_g = row80 + (a * 64 - 8)
@@ -303,13 +312,11 @@
 
     pair_ez, pair_hx, pair_hy = ((HE[k] * ok_m, sides(k) * ok_s) for k in range(3))
 
-    def coef80(table, ids, ok):
-        parts = [pick(table, ids[8 * r : 8 * r + 8, :].astype(i32)) for r in range(10)]
-        return jnp.concatenate(parts, axis=0) * ok
-
-    ids_m, ids_s = HE[3], sides(3)
-    pair_damp = (coef80(damp1(), ids_m, ok_m), coef80(damp1(), ids_s, ok_s))
-    pair_gain = (coef80(gain1(), ids_m, ok_m), coef80(gain1(), ids_s, ok_s))
+    ids_s = sides(3)
+    sides_dg = [coef_rows(ids_s[8 * r : 8 * r + 8, :]) for r in range(10)]
+    pair_damp, pair_gain = (
+        (DG[k] * ok_m, jnp.concatenate([part[k] for part in sides_dg], axis=0) * ok_s) for k in range(2)
+    )
 
     def right_of(x):
         m, s = pltpu.roll(x[0], 127, 1), pltpu.roll(x[1], 127, 1)
@@ -373,11 +380,10 @@
 
     exchange(1, S2, R2, 8, 2)
 
-    loads[6].wait()
+    to_cells(FE, put_in(WE))
     to_cells(FX, put_in(WX))
-    loads[7].wait()
     to_cells(FY, put_in(WY))
-    received(0, R1, 9).wait()
+    received(0, 9).wait()
 
     def from1(k):
         return tuple(R1[pl.ds(2 * k + h, 32, stride=16), :] for h in range(2))
@@ -404,7 +410,7 @@
         CO[4, pl.ds(32 * h, 32), :] = f_mid[h]
 
     def co_rows(tg, h):
-        return pl.ds(pl.multiple_of(32 * h + 8 * tg, 8), 8)
+        return aligned(32 * h + 8 * tg, 8)
 
     def prepare(tg, carry):
         halves = [(2.0 * CO[0, co_rows(tg, h), :], CO[4, co_rows(tg, h), :]) for h in range(2)]
@@ -419,8 +425,12 @@
 
     lax.fori_loop(0, 4, prepare, 0)
 
-    def substep(k, carry):
-        m, tg = k // 4, lax.rem(k, 4)
+    def substeps(m, carry):
+        for tg in range(4):
+            substep(m, tg)
+        return carry
+
+    def substep(m, tg):
         half_box = [CO[0, co_rows(tg, h), :] for h in range(2)]
         rim = [CO[1 + m, co_rows(tg, h), :] for h in range(2)]
         e = [WE[cell_rows(tg, u), :] for u in range(18)]
@@ -452,14 +462,12 @@
             electric(p - 1)
         electric(4)
         electric(5)
-        return carry
-
-    def means(tg, carry):
+
+    def means(tg):
         for h in range(2):
             part = [WE[cell_rows(tg, u), :] for u in range(9 * h, 9 * h + 9)]
             total = ((part[0] + part[1]) + (part[2] + part[3])) + ((part[4] + part[5]) + (part[6] + part[7])) + part[8]
             CO[5, co_rows(tg, h), :] = total * (1.0 / 9.0)
-        return carry
 
     edge_col = (col_in == 0) | (col_in == 15)
     frame = (edge_col | (rows_in[0] == 0), edge_col | (rows_in[1] == 15))
@@ -506,10 +514,6 @@
             hx = tuple(jnp.where(col_in == 15, w2[h], hx[h]) for h in range(2))
             hy_up = (jnp.where(rows_in[0] == 0, w1[0], hy_up[0]), hy_up[1])
             hx_left = tuple(jnp.where(col_in == 0, w2[h], hx_left[h]) for h in range(2))
-            for h in range(2):
-                O1[pl.ds(h, 32, stride=8), :] = hx[h]
-                O1[pl.ds(2 + h, 32, stride=8), :] = hy[h]
-            exchange(2, O1, RO1, 8, 4)
         drive = []
         for h in range(2):
             total = jnp.zeros((32, 128), f32)
@@ -526,10 +530,11 @@
             share = (m + 1) / 3.0
             for h in range(2):
                 CO[1 + m, pl.ds(32 * h, 32), :] = f_rim[h] * ((1.0 - share) * ez[h] + share * new[h])
-        lax.fori_loop(0, 12, substep, 0)
-        lax.fori_loop(0, 4, means, 0)
+        lax.fori_loop(0, 3, substeps, 0)
+        for tg in range(4):
+            means(tg)
         if n == 0:
-            received(1, R2, 2).wait()
+            received(1, 2).wait()
         if n < 2:
             rim = R2[pl.ds(0, 32, stride=8), :]
             out = []
@@ -555,25 +560,26 @@
         pltpu.make_async_remote_copy(
             src_ref=TS.at[pl.ds(0, 3), :],
             dst_ref=TB.at[pl.ds(pl.multiple_of(8 * b, 8), 3), :],
-            send_sem=send_sem.at[4], recv_sem=recv_sem.at[4],
+            send_sem=send_sem, recv_sem=recv_sem.at[4],
             device_id=dev(a, n), device_id_type=MESH,
         ).start()
     TB[pl.ds(pl.multiple_of(8 * b, 8), 3), :] = TS[pl.ds(0, 3), :]
 
-    for h in range(2):
-        O2[pl.ds(h, 32, stride=8), :] = ez[h]
-    exchange(3, O2, RO2, 8, 2)
+    for k, field in enumerate((ez, hx, hy)):
+        for h in range(2):
+            O1[pl.ds(2 * k + h, 32, stride=8), :] = field[h]
+    exchange(2, O1, RO1, 8, 6)
 
     from_cells(WE, FE)
     from_cells(WX, FX)
     seven = (NB - 1) * 3
-    pltpu.make_async_copy(TB.at[pl.ds(0, seven), :], TB.at[pl.ds(0, seven), :], recv_sem.at[4]).wait()
+    bytes_of(seven, recv_sem.at[4]).wait()
     for n in range(STEPS):
         TS2[pl.ds(n, 1), :] = jnp.sum(TB[pl.ds(n, 8, stride=8), :], axis=0, keepdims=True)
-    exchange(5, TS2, TG, 8, 3, same=True)
+    exchange(3, TS2, TG, 8, 3, same=True)
 
     from_cells(WY, FY)
-    received(2, RO1, 4).wait()
+    received(2, 6).wait()
 
     def unpack(src, first, dst):
         for ci in range(4):
@@ -581,17 +587,14 @@
                 x = src[pl.ds(ci * 64 + first + h, 8, stride=8), :]
                 dst[pl.ds(16 * ci + h, 8, stride=2), :] = swap_blocks(x, sub, lg)
 
-    unpack(RO1, 0, hx_out)
-    unpack(RO1, 2, hy_out)
-    received(3, RO2, 2).wait()
-    unpack(RO2, 0, ez_out)
-    received(5, TG, 3).wait()
+    unpack(RO1, 0, ez_out)
+    unpack(RO1, 2, hx_out)
+    unpack(RO1, 4, hy_out)
+    received(3, 3).wait()
     for n in range(STEPS):
         tr_out[pl.ds(n, 1), :] = jnp.sum(TG[pl.ds(n, 32, stride=8), :], axis=0, keepdims=True)
 
-    for j, buf, rows in ((0, S1, 9), (1, S2, 2), (2, O1, 4), (3, O2, 2), (5, TG, 3)):
-        sent(j, buf, rows).wait()
-    pltpu.make_async_copy(TB.at[pl.ds(0, seven), :], TB.at[pl.ds(0, seven), :], send_sem.at[4]).wait()
+    bytes_of(224 + (NA - 1) * (9 + 2 + 6 + 3) + seven, send_sem).wait()
 
 
 def finish(*refs):
@@ -626,16 +629,16 @@
         in_specs=[anywhere] * 14,
         out_specs=(vmem,) * 7,
         scratch_shapes=[
-            v(4, 80, 128), v(64, 128, dtype=i32), v(64, 128), v(80, 128), v(80, 128), v(4, 64, 128),
+            v(4, 80, 128), v(2, 80, 128), v(64, 128, dtype=i32), v(64, 128), v(80, 128), v(80, 128), v(4, 64, 128),
             v(512, 128), v(512, 128), v(256, 128), v(256, 128),
-            v(256, 128), v(256, 128), v(256, 128), v(256, 128),
+            v(256, 128), v(256, 128),
             v(8, 128), v(64, 128), v(8, 128), v(256, 128),
             v(576, 128, dtype=i32), v(584, 128), v(584, 128),
             v(584, 128), v(584, 128), v(584, 128),
             v(144, 128, dtype=i32), v(144, 128, dtype=i32), v(272, 128), v(6, 64, 128),
             v(4, 32, dtype=i32), pltpu.SMEM((1, 4), i32), pltpu.SMEM((3, 4), f32),
             v(1, 128, dtype=i32), v(1, 8), v(1, 8),
-            dma(14), dma(8), dma(8), dma(6), dma(6), pltpu.SemaphoreType.REGULAR,
+            v(2304, 128), dma(8), pltpu.SemaphoreType.DMA, pltpu.SemaphoreType.DMA, dma(5), pltpu.SemaphoreType.REGULAR,
         ],
         compiler_params=pltpu.CompilerParams(collective_id=0, has_side_effects=True),
     )(

time: 38 us -> 34.8 us (0.916)
  Pallas kernels: 37.2 us -> 34 us
    pallas_call x1, Pallas kernels: 36.2 us -> 33 us  [shards(): pl.pallas_call(kernel, name='nested', out_shape=tuple((pltpu.VMEM(shape,...]
where the time goes in v3:
time: 34.8 us; the launch traced here: 34.7 us
  Pallas kernels  34 us (98%)
  between operations  0.65 us (2%)
    pallas_call x1, Pallas kernels, shards(): pl.pallas_call(kernel, name='nested', out_shape=tuple((pltpu.VMEM(shape,...  33 us
    pallas_call x1, Pallas kernels, shards(): pl.pallas_call(finish, name='finish', out_shape=tuple((jax.ShapeDtypeStru...  1.01 us

profile of v3, /device:TPU:1, one launch (start us, length us, event | category | flops | bytes accessed | tf_op | source)
XLA Modules:
  0.0 34.7 jit_solution(13766041842898835167)
XLA Ops:
  0.6 33.0 %nested.1 = (f32[64,128]{1,0:T(8,128)S(1)}, f32[64,128]{1,0:T(8,128)S(1)}, f32[64,128]{1,0:T(8,128)S(1)}, f32[576,128]{1,0:T(8,128)S(1)}, f32[576,128]{1,0:T(8,1...) custom-call(f32[64,128]{1,0:T(8,128)} %ez_in.1, f32[64,128]{1,0:T(8,128)} %hx_in.1, f32[64,128]{1,0:T(8,128)} %hy_in.1, ...), custom_call_target="tpu_custom_call" | custom-call | tf_op jit(solution)/shard_map/nested/pallas_call | solution.py:625
  33.7 1.0 %finish.1 = (f32[64,128]{1,0:T(8,128)}, f32[64,128]{1,0:T(8,128)}, f32[64,128]{1,0:T(8,128)}, f32[576,128]{1,0:T(8,128)}, f32[576,128]{1,0:T(8,128)}, /*index=5*/f32[576,128]{1,0:T(8,128)}, f32[3,128]{1,0:T(4,128)}) custom-call(f32[64,128]{1,0:T(8,128)S(1)} %get-tuple-element.21.refs_0_, f32[64,128]{1,0:T(8,128)S(1)} %get-tuple-element.22.refs_1_, ...), custom_call_target="tpu_custom_call" | custom-call | tf_op jit(solution)/shard_map/finish/pallas_call | solution.py:650

commit v4 on v3

--- a/solution.py
+++ b/solution.py
@@ -23,15 +23,8 @@
     return lax.broadcasted_iota(i32, (8, 128), 0)
 
 
-def swap_blocks(x, sub, lg):
-    for k in range(3):
-        bs = (sub >> k) & 1
-        bl = (lg >> k) & 1
-        step = 16 << k
-        down = pltpu.roll(pltpu.roll(x, 1 << k, 0), 128 - step, 1)
-        up = pltpu.roll(pltpu.roll(x, 8 - (1 << k), 0), step, 1)
-        x = jnp.where(bs == bl, x, jnp.where(bs == 1, down, up))
-    return x
+def swap_blocks(x, turn, pick_rows, back):
+    return lane_gather(jnp.take_along_axis(lane_gather(x, turn), pick_rows, axis=0), back)
 
 
 def lane_gather(x, idx):
@@ -76,7 +69,7 @@
     ez_out, hx_out, hy_out, fez_out, fhx_out, fhy_out, tr_out,
     HE, DG, IDS, PB, PEL, PER, E2, S1, R1, S2, R2, O1, RO1, TS, TB, TS2, TG,
     FI, FD, FG, WE, WX, WY, IDX, SEL, TAB, CO, BOX, SRC, WAVE, RCV, EPS, SIG,
-    MANY, in_sem, halo_sem, send_sem, recv_sem, stage_sem,
+    MANY, in_sem, halo_sem, send_sem, recv_sem, stage_sem, far_sem,
 ):
     FE, FX, FY = fez_out, fhx_out, fhy_out
     grp = lax.axis_index("grp")
@@ -120,12 +113,14 @@
         pl.semaphore_signal(barrier, inc=1, device_id=dev(na, nb), device_id_type=MESH)
 
     y, z = a // 8, lax.rem(a, 8)
+    for d in (4, 3, 5, 2, 6):
+        signal(y * 8 + lax.rem(z + d, 8), b)
     for na in (am, ap):
         for nb in (bm, b, bp):
             signal(na, nb)
-    for d in range(1, NB):
-        signal(a, lax.rem(b + d, NB))
-    for d in range(1, 8):
+    signal(a, bm)
+    signal(a, bp)
+    for d in (1, 7):
         signal(y * 8 + lax.rem(z + d, 8), b)
     y_peers = [lax.rem(y + d, 4) * 8 + z for d in range(1, 4)]
     for n in y_peers:
@@ -134,6 +129,11 @@
     lane = lanes()
     sub = sublanes()
     lg = lane >> 4
+    swap = (
+        (((lg + sub) & 7) << 4) + (lane & 15),
+        (sub - lg) & 7,
+        (((sub - lg) & 7) << 4) + (lane & 15),
+    )
 
     for g in range(18):
         pos = lane + 128 * g
@@ -201,7 +201,7 @@
         ci, h = v // 2, v % 2
         for k in range(4):
             x = HE[k, pl.ds(8 + 16 * ci + h, 8, stride=2), :]
-            S1[pl.ds(ci * 128 + 2 * k + h, 8, stride=16), :] = swap_blocks(x, sub, lg)
+            S1[pl.ds(ci * 128 + 2 * k + h, 8, stride=16), :] = swap_blocks(x, *swap)
     row32 = lax.broadcasted_iota(i32, (32, 32), 0)
     col32 = lax.broadcasted_iota(i32, (32, 32), 1)
     lane32 = lax.broadcasted_iota(i32, (32, 128), 1)
@@ -239,7 +239,7 @@
         FD[cell_rows(tg, u), :] = pick(damp3(), ids)
         FG[cell_rows(tg, u), :] = pick(gain3(), ids)
 
-    pl.semaphore_wait(barrier, 6 + (NB - 1) + 7 + 3)
+    pl.semaphore_wait(barrier, 6 + 2 + 7 + 3)
     for n in y_peers:
         pl.semaphore_signal(stage_sem, inc=1, device_id=dev(n, b), device_id_type=MESH)
 
@@ -285,6 +285,13 @@
     to_cells(FI, put_coef)
     pl.semaphore_wait(stage_sem, 3)
     exchange(0, S1, R1, 16, 9)
+
+    def tell(j, d):
+        for n in (lax.rem(b + NB - d, NB), lax.rem(b + d, NB)):
+            pl.semaphore_signal(far_sem.at[j], inc=1, device_id=dev(a, n), device_id_type=MESH)
+
+    tell(0, 1)
+    to_cells(FE, put_in(WE))
 
     def coef_rows(ids):
         ids = ids.astype(i32)
@@ -373,14 +380,15 @@
             halves = []
             for h in range(2):
                 x = E2[k, pl.ds(16 * ci + h, 8, stride=2), :]
-                halves.append(lane_gather(swap_blocks(x, sub, lg), frame_idx))
+                halves.append(lane_gather(swap_blocks(x, *swap), frame_idx))
             got.append(jnp.where(from_h1, halves[1], halves[0]))
         S2[pl.ds(ci * 64, 8, stride=8), :] = jnp.where(lane < 64, got[0], got[1])
         S2[pl.ds(ci * 64 + 1, 8, stride=8), :] = jnp.where((lane & 63) < 32, got[2], got[3])
 
     exchange(1, S2, R2, 8, 2)
 
-    to_cells(FE, put_in(WE))
+    pl.semaphore_wait(far_sem.at[0], 2)
+    tell(1, 2)
     to_cells(FX, put_in(WX))
     to_cells(FY, put_in(WY))
     received(0, 9).wait()
@@ -530,7 +538,8 @@
             share = (m + 1) / 3.0
             for h in range(2):
                 CO[1 + m, pl.ds(32 * h, 32), :] = f_rim[h] * ((1.0 - share) * ez[h] + share * new[h])
-        lax.fori_loop(0, 3, substeps, 0)
+        for m in range(3):
+            substeps(m, 0)
         for tg in range(4):
             means(tg)
         if n == 0:
@@ -555,6 +564,7 @@
                 picked = picked + jnp.where((r_tile == sub + 8 * q) & (r_half == h), got, 0.0)
         TS[pl.ds(n, 1), :] = jnp.sum(picked, axis=0, keepdims=True)
 
+    pl.semaphore_wait(far_sem.at[1], 2)
     for d in range(1, NB):
         n = lax.rem(b + d, NB)
         pltpu.make_async_remote_copy(
@@ -585,7 +595,7 @@
         for ci in range(4):
             for h in range(2):
                 x = src[pl.ds(ci * 64 + first + h, 8, stride=8), :]
-                dst[pl.ds(16 * ci + h, 8, stride=2), :] = swap_blocks(x, sub, lg)
+                dst[pl.ds(16 * ci + h, 8, stride=2), :] = swap_blocks(x, *swap)
 
     unpack(RO1, 0, ez_out)
     unpack(RO1, 2, hx_out)
@@ -638,7 +648,7 @@
             v(144, 128, dtype=i32), v(144, 128, dtype=i32), v(272, 128), v(6, 64, 128),
             v(4, 32, dtype=i32), pltpu.SMEM((1, 4), i32), pltpu.SMEM((3, 4), f32),
             v(1, 128, dtype=i32), v(1, 8), v(1, 8),
-            v(2304, 128), dma(8), pltpu.SemaphoreType.DMA, pltpu.SemaphoreType.DMA, dma(5), pltpu.SemaphoreType.REGULAR,
+            v(2304, 128), dma(8), pltpu.SemaphoreType.DMA, pltpu.SemaphoreType.DMA, dma(5), pltpu.SemaphoreType.REGULAR, pltpu.SemaphoreType.REGULAR((2,)),
         ],
         compiler_params=pltpu.CompilerParams(collective_id=0, has_side_effects=True),
     )(

time: 34.8 us -> 34.3 us (0.986)
  Pallas kernels: 34 us -> 33.5 us
    pallas_call x1, Pallas kernels: 33 us -> 32.5 us  [shards(): pl.pallas_call(kernel, name='nested', out_shape=tuple((pltpu.VMEM(shape,...]
where the time goes in v4:
time: 34.3 us; the launch traced here: 34.2 us
  Pallas kernels  33.5 us (98%)
  between operations  0.65 us (2%)
    pallas_call x1, Pallas kernels, shards(): pl.pallas_call(kernel, name='nested', out_shape=tuple((pltpu.VMEM(shape,...  32.5 us
    pallas_call x1, Pallas kernels, shards(): pl.pallas_call(finish, name='finish', out_shape=tuple((jax.ShapeDtypeStru...  1.01 us

profile of v4, /device:TPU:1, one launch (start us, length us, event | category | flops | bytes accessed | tf_op | source)
XLA Modules:
  0.0 34.2 jit_solution(3292725982162614204)
XLA Ops:
  0.6 32.5 %nested.1 = (f32[64,128]{1,0:T(8,128)S(1)}, f32[64,128]{1,0:T(8,128)S(1)}, f32[64,128]{1,0:T(8,128)S(1)}, f32[576,128]{1,0:T(8,128)S(1)}, f32[576,128]{1,0:T(8,1...) custom-call(f32[64,128]{1,0:T(8,128)} %ez_in.1, f32[64,128]{1,0:T(8,128)} %hx_in.1, f32[64,128]{1,0:T(8,128)} %hy_in.1, ...), custom_call_target="tpu_custom_call" | custom-call | tf_op jit(solution)/shard_map/nested/pallas_call | solution.py:635
  33.2 1.0 %finish.1 = (f32[64,128]{1,0:T(8,128)}, f32[64,128]{1,0:T(8,128)}, f32[64,128]{1,0:T(8,128)}, f32[576,128]{1,0:T(8,128)}, f32[576,128]{1,0:T(8,128)}, /*index=5*/f32[576,128]{1,0:T(8,128)}, f32[3,128]{1,0:T(4,128)}) custom-call(f32[64,128]{1,0:T(8,128)S(1)} %get-tuple-element.21.refs_0_, f32[64,128]{1,0:T(8,128)S(1)} %get-tuple-element.22.refs_1_, ...), custom_call_target="tpu_custom_call" | custom-call | tf_op jit(solution)/shard_map/finish/pallas_call | solution.py:660

commit v5 on v4

--- a/solution.py
+++ b/solution.py
@@ -67,7 +67,7 @@
 def kernel(
     ez_in, hx_in, hy_in, ids_in, eps_in, sig_in, fez_in, fhx_in, fhy_in, fids_in, box_in, src_in, wave_in, rcv_in,
     ez_out, hx_out, hy_out, fez_out, fhx_out, fhy_out, tr_out,
-    HE, DG, IDS, PB, PEL, PER, E2, S1, R1, S2, R2, O1, RO1, TS, TB, TS2, TG,
+    HE, DG, IDS, PB, QL, QR, PEL, PER, E2, S1, R1, S2, R2, O1, RO1, TS, TB, TS2, TG,
     FI, FD, FG, WE, WX, WY, IDX, SEL, TAB, CO, BOX, SRC, WAVE, RCV, EPS, SIG,
     MANY, in_sem, halo_sem, send_sem, recv_sem, stage_sem, far_sem,
 ):
@@ -218,7 +218,12 @@
         near = (lane64 - 8 * k) & 127
         x = HE[k, pl.ds(8, 64), :]
         packed = jnp.where((near < 3) | (near >= 125), pltpu.roll(x, 8 * k, 1) if k else x, packed)
-    PB[...] = packed
+    packed = jnp.where(lane64 < 29, packed, pltpu.roll(packed, 32, 1))
+    quarter = lane64[0:16, :] >> 5
+    small = packed[0:16, :]
+    for k in range(1, 4):
+        small = jnp.where(quarter == k, pltpu.roll(packed[16 * k : 16 * k + 16, :], 32 * k, 1), small)
+    PB[...] = small
 
     TAB[pl.ds(0, 8), :] = jnp.ones((8, 128), f32)
     TAB[pl.ds(8, 8), :] = jnp.zeros((8, 128), f32)
@@ -252,12 +257,12 @@
 
     halo(HE.at[:, pl.ds(64, 8), :], HE.at[:, pl.ds(0, 8), :], ap, b)
     halo(HE.at[:, pl.ds(8, 8), :], HE.at[:, pl.ds(72, 8), :], am, b)
-    halo(PB, PEL.at[pl.ds(8, 64), :], a, bp)
-    halo(PB, PER.at[pl.ds(8, 64), :], a, bm)
-    halo(PB.at[pl.ds(56, 8), :], PEL.at[pl.ds(0, 8), :], ap, bp)
-    halo(PB.at[pl.ds(56, 8), :], PER.at[pl.ds(0, 8), :], ap, bm)
-    halo(PB.at[pl.ds(0, 8), :], PEL.at[pl.ds(72, 8), :], am, bp)
-    halo(PB.at[pl.ds(0, 8), :], PER.at[pl.ds(72, 8), :], am, bm)
+    halo(PB, QL.at[pl.ds(8, 16), :], a, bp)
+    halo(PB, QR.at[pl.ds(8, 16), :], a, bm)
+    halo(PB.at[pl.ds(8, 8), :], QL.at[pl.ds(0, 8), :], ap, bp)
+    halo(PB.at[pl.ds(8, 8), :], QR.at[pl.ds(0, 8), :], ap, bm)
+    halo(PB.at[pl.ds(0, 8), :], QL.at[pl.ds(24, 8), :], am, bp)
+    halo(PB.at[pl.ds(0, 8), :], QR.at[pl.ds(24, 8), :], am, bm)
 
     def ring(d, size):
         return min(d, size - d)
@@ -299,7 +304,13 @@
 
     for r in range(1, 9):
         DG[0, pl.ds(8 * r, 8), :], DG[1, pl.ds(8 * r, 8), :] = coef_rows(HE[3, pl.ds(8 * r, 8), :])
-    bytes_of(2 * 32 + 2 * 64 + 4 * 8, halo_sem).wait()
+    bytes_of(2 * 32 + 2 * 16 + 4 * 8, halo_sem).wait()
+    for small, wide in ((QL, PEL), (QR, PER)):
+        wide[pl.ds(0, 8), :] = pltpu.roll(small[pl.ds(0, 8), :], 32, 1)
+        wide[pl.ds(72, 8), :] = small[pl.ds(24, 8), :]
+        for k in range(4):
+            x = small[pl.ds(8, 16), :]
+            wide[pl.ds(8 + 16 * k, 16), :] = pltpu.roll(x, 128 - 32 * k, 1) if k else x
     for r in (0, 9):
         DG[0, pl.ds(8 * r, 8), :], DG[1, pl.ds(8 * r, 8), :] = coef_rows(HE[3, pl.ds(8 * r, 8), :])
     lane80 = lax.broadcasted_iota(i32, (80, 128), 1)
@@ -315,6 +326,8 @@
         left, right = PEL[...], PER[...]
         if k:
             left, right = pltpu.roll(left, 128 - 8 * k, 1), pltpu.roll(right, 128 - 8 * k, 1)
+        else:
+            left = pltpu.roll(left, 96, 1)
         return jnp.where(lane80 >= 125, left, jnp.where(lane80 < 3, right, 0.0))
 
     pair_ez, pair_hx, pair_hy = ((HE[k] * ok_m, sides(k) * ok_s) for k in range(3))
@@ -604,7 +617,7 @@
     for n in range(STEPS):
         tr_out[pl.ds(n, 1), :] = jnp.sum(TG[pl.ds(n, 32, stride=8), :], axis=0, keepdims=True)
 
-    bytes_of(224 + (NA - 1) * (9 + 2 + 6 + 3) + seven, send_sem).wait()
+    bytes_of(128 + (NA - 1) * (9 + 2 + 6 + 3) + seven, send_sem).wait()
 
 
 def finish(*refs):
@@ -639,7 +652,8 @@
         in_specs=[anywhere] * 14,
         out_specs=(vmem,) * 7,
         scratch_shapes=[
-            v(4, 80, 128), v(2, 80, 128), v(64, 128, dtype=i32), v(64, 128), v(80, 128), v(80, 128), v(4, 64, 128),
+            v(4, 80, 128), v(2, 80, 128), v(64, 128, dtype=i32),
+            v(16, 128), v(32, 128), v(32, 128), v(80, 128), v(80, 128), v(4, 64, 128),
             v(512, 128), v(512, 128), v(256, 128), v(256, 128),
             v(256, 128), v(256, 128),
             v(8, 128), v(64, 128), v(8, 128), v(256, 128),

time: 34.3 us -> 34.3 us (level)
  no operation moved by 1% of the time
where the time goes in v5:
time: 34.3 us; the launch traced here: 34.2 us
  Pallas kernels  33.6 us (98%)
  between operations  0.65 us (2%)
    pallas_call x1, Pallas kernels, shards(): pl.pallas_call(kernel, name='nested', out_shape=tuple((pltpu.VMEM(shape,...  32.6 us
    pallas_call x1, Pallas kernels, shards(): pl.pallas_call(finish, name='finish', out_shape=tuple((jax.ShapeDtypeStru...  1.01 us

profile of v5, /device:TPU:1, one launch (start us, length us, event | category | flops | bytes accessed | tf_op | source)
XLA Modules:
  0.0 34.2 jit_solution(116149048107409901)
XLA Ops:
  0.6 32.6 %nested.1 = (f32[64,128]{1,0:T(8,128)S(1)}, f32[64,128]{1,0:T(8,128)S(1)}, f32[64,128]{1,0:T(8,128)S(1)}, f32[576,128]{1,0:T(8,128)S(1)}, f32[576,128]{1,0:T(8,1...) custom-call(f32[64,128]{1,0:T(8,128)} %ez_in.1, f32[64,128]{1,0:T(8,128)} %hx_in.1, f32[64,128]{1,0:T(8,128)} %hy_in.1, ...), custom_call_target="tpu_custom_call" | custom-call | tf_op jit(solution)/shard_map/nested/pallas_call | solution.py:648
  33.2 1.0 %finish.1 = (f32[64,128]{1,0:T(8,128)}, f32[64,128]{1,0:T(8,128)}, f32[64,128]{1,0:T(8,128)}, f32[576,128]{1,0:T(8,128)}, f32[576,128]{1,0:T(8,128)}, /*index=5*/f32[576,128]{1,0:T(8,128)}, f32[3,128]{1,0:T(4,128)}) custom-call(f32[64,128]{1,0:T(8,128)S(1)} %get-tuple-element.21.refs_0_, f32[64,128]{1,0:T(8,128)S(1)} %get-tuple-element.22.refs_1_, ...), custom_call_target="tpu_custom_call" | custom-call | tf_op jit(solution)/shard_map/finish/pallas_call | solution.py:674
